TPU v7x, 128 devices: a whole 4x4x4 slice. The times are simulated.
128 devices in a mesh: dev: 128 (over y, x, z, core).
Axes of the slice: x: 4, y: 4, z: 4, core: 2. Of those that a mesh axis runs over, the one named last changes fastest.
Arguments:
- dual_blocks: bfloat16 [128, 3072, 3072], P('dev'), as said below
- rigid_modes: float32 [128, 6, 3072], P('dev'), may hold values from -5 to 5
- dual_local: float32 [128, 8, 3072], P('dev'), may hold values from -6 to 6
- coarse_rhs: float32 [128, 6, 8], P('dev'), may hold values from -4608 to 4608
- iface_sizes: int32 [128], P('dev'), may hold values from 1536 to 3072, as said below
- neighbours: int32 [128, 6], P('dev'), may hold values from -1 to 127, as said below
- shared_counts: int32 [128, 6], P('dev'), may hold values from 256 to 512, as said below
- iface_map: int32 [128, 3072], P('dev'), may hold values from -1 to 3071, as said below
- owner: int32 [128], replicated, may hold values from 0 to 127, as said below
Outputs:
- multipliers: float32 [128, 8, 3072], P('dev')
- projected_residual: float32 [128, 8, 3072], P('dev')
Inputs may be any that keep to these rules, and one draw needn't show every extreme that they name: `dual_blocks`: each block is symmetric positive definite, and so is each of its leading principal parts. Grid subdomain g is held by slot owner[g] = (g + s) mod 128 for one offset s of the draw, so the subdomains across the faces -x, +x, -y, +y, -z, +z of slot i sit in slots i - 1, i + 1, i - 4, i + 4, i - 16, i + 16, taken mod 128. `neighbours`: the subdomains form a grid of 4 x 4 x 128/16 with g = x + 4 y + 16 z. Row i lists, for the faces -x, +x, -y, +y, -z, +z of the subdomain held in slot i, the grid subdomain across that face, or -1 on the outer boundary; across a face from g the opposite face names g. `shared_counts`: equal on both sides of a shared face; some subdomain has 512 on all its faces. `iface_sizes`: the sum of the slot's shared_counts row; some subdomain has 3072. `iface_map`: for j < iface_sizes[i], entry j is f * 512 + p for the dof at position p of face f of slot i (p below that face's count), each such code once; -1 beyond. The dof at position p of a shared face pairs with the dof at position p of the opposite face of the neighbour.
All inputs are finite; a program needn't handle non-finite values.
Results may differ from a plain program's by a relative error of at most 0.025.
Values sent between devices are 32-bit elements; how exact they have to be, the bound alone decides.
A program may use at most 128 MiB of HBM per device.

v0:
```python
import math

import jax
import jax.numpy as jnp
from jax import lax
from jax.sharding import Mesh
from jax.sharding import PartitionSpec as P

FACES = 6
MODES = 6
CAP = 512
NMAX = 3072
ITERS = 3
DEV = ("dev_0", "dev_1", "dev_2", "dev_3")


HIGHEST_PRECISION = lax.Precision.HIGHEST
OPPOSITE = (1, 0, 3, 2, 5, 4)
FACE_STEPS = (-1, 1, -4, 4, -16, 16)


def from_behind(value, axis, by):
    length = lax.axis_size(axis)
    return lax.ppermute(value, axis, [(i, (i + by) % length) for i in range(length)])


def sent_together(arrays, axis, dim, along):
    widths = [math.prod(a.shape[along:]) for a in arrays]
    both = jnp.concatenate(
        [a.reshape(*a.shape[:along], w) for a, w in zip(arrays, widths)], axis=along
    )
    out = lax.all_gather(both, axis, axis=dim, tiled=True)
    parts = jnp.split(out, [sum(widths[:k]) for k in range(1, len(widths))], axis=along)
    return tuple((b.reshape(*out.shape[:along], *a.shape[along:]) for a, b in zip(arrays, parts)))


def one_axis_at_a_time(value, axes):
    for axis in axes:
        value = lax.psum(value, axis)
    return value


def solve_coarse(factor, vector):
    middle = lax.linalg.triangular_solve(factor, vector, left_side=True, lower=True)
    return lax.linalg.triangular_solve(factor, middle, left_side=True, lower=True, transpose_a=True)


def per_device(
    dual_blocks,
    rigid_modes,
    dual_local,
    coarse_rhs,
    iface_sizes,
    neighbours,
    shared_counts,
    iface_map,
    owner,
):
    my_slot = lax.axis_index(DEV)
    devices = lax.axis_size(DEV)
    loads = dual_local.shape[1]
    columns = jnp.arange(NMAX, dtype=jnp.int32)
    live_dofs = columns < iface_sizes[0]
    dof_codes = jnp.clip(jnp.where(live_dofs, iface_map[0], 0), 0, FACES * CAP - 1)
    which_face = dof_codes // CAP
    position = dof_codes % CAP
    face_row = neighbours[0]
    count_row = shared_counts[0]
    face_onehot = which_face[None, :] == jnp.arange(FACES, dtype=jnp.int32)[:, None]
    has_partner = jnp.any(face_onehot & (face_row >= 0)[:, None], axis=0)
    face_limit = jnp.sum(jnp.where(face_onehot, count_row[:, None], 0), axis=0)
    shared = live_dofs & has_partner & (position < face_limit)
    live_float = live_dofs.astype(jnp.float32)
    shared_float = shared.astype(jnp.float32)
    weights = jnp.where(shared, 0.5, live_float)
    targets = jnp.where(live_dofs, dof_codes, FACES * CAP)
    inverse = (
        jnp.full((FACES * CAP,), NMAX, jnp.int32)
        .at[targets]
        .set(columns, mode="drop")
        .reshape(FACES, CAP)
    )
    partner_slot = jnp.where(face_row >= 0, owner[jnp.clip(face_row, 0, owner.shape[0] - 1)], 0)
    face_mask = (
        (face_row >= 0)[:, None] & (jnp.arange(CAP, dtype=jnp.int32)[None, :] < count_row[:, None])
    ).astype(jnp.float32)

    def gather_faces(values):
        padded = jnp.concatenate([values, jnp.zeros((values.shape[0], 1), values.dtype)], axis=1)
        return jnp.take(padded, inverse, axis=1)

    def across_faces(face_vals, mover):
        pieces = [mover(face_vals[:, OPPOSITE[face]], -FACE_STEPS[face]) for face in range(FACES)]
        return jnp.stack(pieces, axis=1) * face_mask[None]

    def spread_back(far_faces):
        flattened = far_faces.reshape(far_faces.shape[0], FACES * CAP)
        return jnp.take(flattened, dof_codes, axis=1) * shared_float[None]

    def combine(values, far_faces):
        return live_float[None] * (values - spread_back(far_faces))

    def partial_inner(left_vec, right_vec):
        return jnp.sum(weights[None] * left_vec * right_vec, axis=1)

    modes_live = rigid_modes[0] * live_float[None]
    local_rhs = dual_local[0]
    own_modes = gather_faces(modes_live)
    own_rhs = gather_faces(local_rhs)
    setup_pieces = [
        from_behind(
            (own_modes[:, OPPOSITE[face]], own_rhs[:, OPPOSITE[face]]), DEV, -FACE_STEPS[face]
        )
        for face in range(FACES)
    ]
    far_modes = jnp.stack([piece[0] for piece in setup_pieces], axis=1) * face_mask[None]
    far_rhs = jnp.stack([piece[1] for piece in setup_pieces], axis=1) * face_mask[None]
    dual_rhs = combine(local_rhs, far_rhs)
    diagonal = lax.dot_general(
        modes_live, modes_live, (((1,), (1,)), ((), ())), precision=HIGHEST_PRECISION
    )
    coupling = -jnp.einsum("afp,bfp->afb", own_modes, far_modes, precision=HIGHEST_PRECISION)
    block_row = jnp.zeros((MODES, devices, MODES), jnp.float32).at[:, my_slot, :].set(diagonal)
    block_row = block_row.at[:, partner_slot, :].add(coupling)
    coarse_matrix, coarse_goal = (
        lax.all_gather(block_row.reshape(MODES, devices * MODES), DEV, axis=0, tiled=True),
        lax.all_gather(coarse_rhs[0], DEV, axis=0, tiled=True),
    )
    factor = jnp.linalg.cholesky(coarse_matrix)

    def modes_apply(solution):
        stacked = solution.reshape(devices, MODES, loads)
        own_part = lax.dot_general(
            stacked[my_slot], modes_live, (((0,), (0,)), ((), ())), precision=HIGHEST_PRECISION
        )
        far_part = jnp.einsum(
            "bfp,fbl->lfp", far_modes, stacked[partner_slot], precision=HIGHEST_PRECISION
        )
        return combine(own_part, far_part)

    def project(residual):
        coarse_part = lax.dot_general(
            modes_live, residual, (((1,), (1,)), ((), ())), precision=HIGHEST_PRECISION
        )
        parts_all, square_parts = sent_together(
            (coarse_part[None], partial_inner(residual, residual)[None]), DEV, 0, 1
        )
        coarse_all = parts_all.reshape(devices * MODES, loads)
        solution = solve_coarse(factor, coarse_all)
        projected = residual - modes_apply(solution)
        norm_sq = jnp.sum(square_parts, axis=0) - jnp.sum(coarse_all * solution, axis=0)
        return (projected, norm_sq)

    def dual_apply(vector):
        products = lax.dot_general(
            vector.astype(jnp.bfloat16),
            dual_blocks[0],
            (((1,), (1,)), ((), ())),
            preferred_element_type=jnp.float32,
        )
        far_part = across_faces(
            gather_faces(products), lambda piece, offset: from_behind(piece, DEV, offset)
        )
        return combine(products, far_part)

    multipliers = modes_apply(solve_coarse(factor, coarse_goal))
    residual = dual_rhs - dual_apply(multipliers)
    projected, norm_sq = project(residual)
    direction = projected
    for step_index in range(ITERS):
        applied = dual_apply(direction)
        curvature = one_axis_at_a_time(partial_inner(direction, applied), DEV)
        step_size = norm_sq / curvature
        multipliers = multipliers + step_size[:, None] * direction
        residual = residual - step_size[:, None] * applied
        projected, norm_next = project(residual)
        direction = projected + (norm_next / norm_sq)[:, None] * direction
        norm_sq = norm_next
    return (multipliers[None], projected[None])


def solution(mesh):
    finer = Mesh(mesh.devices.reshape(4, 4, 4, 2), ("dev_0", "dev_1", "dev_2", "dev_3"))
    in_specs = (
        P(DEV, None, None),
        P(DEV, None, None),
        P(DEV, None, None),
        P(DEV, None, None),
        P(DEV),
        P(DEV, None),
        P(DEV, None),
        P(DEV, None),
        P(),
    )
    out_specs = (P(DEV, None, None), P(DEV, None, None))
    return jax.shard_map(
        per_device, mesh=finer, in_specs=in_specs, out_specs=out_specs, check_vma=False
    )
```

profile of v0, /device:TPU:1, one launch (start us, length us, event | category | flops | bytes accessed | tf_op | source)
XLA Modules:
  0.0 1063.1 jit_solution(3535072408166169513)
XLA Ops:
  27.0 12.3 %gather_fusion.1 = f32[3072,6]{1,0:T(8,128)} fusion(f32[6,3073]{0,1:T(8,128)} %concatenate.73, s32[3072]{0:T(1024)S(1)} %broadcast_clamp_fusion.1), kind=kCustom, calls=%fused_computation.16 | custom fusion | bytes 159744 | tf_op jit(solution)/shard_map/jit(_take)/gather | solution.py:90
  69.2 37.3 %all-gather = f32[1,768,8]{2,0,1:T(1,128)S(1)} all-gather(f32[1,6,8]{2,0,1:T(1,128)S(1)} %copy-done.22), channel_id=2, replica_groups=mesh['dev_0'=4,'dev_1'=4,'dev_2'=4,'dev_3'=2] {'dev_0','dev_1','dev_2','..., dimensions={1}, use_global_device_ids=true | all-gather | bytes 24768 | tf_op jit(solution)/shard_map/all_gather | solution.py:127
  122.4 14.2 %all-gather.8.cloned.1.call-done = f32[128,6,768]{2,1,0:T(8,128)} async-done(((f32[1,6,768]{2,1,0:T(8,128)}), f32[128,6,768]{2,1,0:T(8,128)}) %all-gather.8.cloned.1.call-update) | async-done | bytes 2359312 | tf_op jit(solution)/shard_map/all_gather | solution.py:126
  285.1 16.2 %while.21 = (s32[]{:T(128)}, f32[768,768]{1,0:T(8,128)S(1)}, s32[6,2]{0,1:T(2,128)S(1)}, f32[6,128,128]{2,1,0:T(8,128)}, s32[]{:T(128)}) while((s32[]{:T(128)}, f32[768,768]{1,0:T(8,128)S(1)}, s32[6,2]{0,1:T(2,128)S(1)}, f32[6,128,128]{2,1,0:T(8,128)}, s32[]{:T(128)}) %tuple.149), condition=%wide.while_cond.2, body=%wide.while_body.2.sunk | while | flops 2 | bytes 132205 | solution.py:45
  301.2 59.8 %custom-call.63 = f32[6,128,128]{1,2,0:T(8,128)S(1)} custom-call(f32[6,128,128]{2,1,0:T(8,128)} %get-tuple-element.83), custom_call_target="InvertDiagBlocksLowerTriangular" | custom-call | tf_op jit(solution)/shard_map/triangular_solve/custom-call.12 | solution.py:45
  376.1 12.2 %gather_fusion.7 = f32[3072,8]{1,0:T(8,128)} fusion(f32[8,3072]{0,1:T(8,128)} %copy.161, s32[3072]{0:T(1024)S(1)} %get-tuple-element.246), kind=kCustom, calls=%fused_computation.clone | custom fusion | bytes 208896 | tf_op jit(solution)/shard_map/jit(_take)/gather | solution.py:98
  403.7 12.3 %gather_fusion.10 = f32[3072,8]{1,0:T(8,128)} fusion(f32[8,3073]{0,1:T(8,128)} %concatenate.75.clone, s32[3072]{0:T(1024)S(1)} %get-tuple-element.247), kind=kCustom, calls=%fused_computation.11.clone | custom fusion | bytes 208896 | tf_op jit(solution)/shard_map/jit(_take)/gather | solution.py:90
  469.1 12.3 %gather_fusion.9 = f32[3072,8]{1,0:T(8,128)} fusion(f32[8,3072]{0,1:T(8,128)} %get-tuple-element.177, s32[3072]{0:T(1024)S(1)} %get-tuple-element.246), kind=kCustom, calls=%fused_computation.2.clone | custom fusion | bytes 208896 | tf_op jit(solution)/shard_map/jit(_take)/gather | solution.py:98
  483.2 12.2 %gather_fusion.11 = f32[3072,8]{1,0:T(8,128)} fusion(f32[8,3072]{0,1:T(8,128)} %get-tuple-element.178, s32[3072]{0:T(1024)S(1)} %get-tuple-element.246), kind=kCustom, calls=%fused_computation.3.clone | custom fusion | bytes 208896 | tf_op jit(solution)/shard_map/jit(_take)/gather | solution.py:98
  501.7 35.2 %all-gather.2 = f32[128,1,56]{2,1,0:T(1,128)S(1)} all-gather(f32[1,1,56]{2,1,0:T(1,128)S(1)} %maximum_bitcast_fusion), channel_id=1, replica_groups=mesh['dev_0'=4,'dev_1'=4,'dev_2'=4,'dev_3'=2] {'dev_0','dev_1','dev_2','..., dimensions={0}, use_global_device_ids=true | all-gather | bytes 28896 | tf_op jit(solution)/shard_map/all_gather | solution.py:32
  552.4 12.2 %gather_fusion.12 = f32[3072,8]{1,0:T(8,128)} fusion(f32[8,3072]{0,1:T(8,128)} %copy.180, s32[3072]{0:T(1024)S(1)} %get-tuple-element.246), kind=kCustom, calls=%fused_computation.4.clone | custom fusion | bytes 208896 | tf_op jit(solution)/shard_map/jit(_take)/gather | solution.py:98
  579.9 12.3 %gather_fusion.13 = f32[3072,8]{1,0:T(8,128)} fusion(f32[8,3073]{0,1:T(8,128)} %concatenate.77.clone, s32[3072]{0:T(1024)S(1)} %get-tuple-element.247), kind=kCustom, calls=%fused_computation.12.clone | custom fusion | bytes 208896 | tf_op jit(solution)/shard_map/jit(_take)/gather | solution.py:90
  617.6 12.2 %gather_fusion.14 = f32[3072,8]{1,0:T(8,128)} fusion(f32[8,3072]{0,1:T(8,128)} %bitcast_multiply_fusion.2, s32[3072]{0:T(1024)S(1)} %get-tuple-element.246), kind=kCustom, calls=%fused_computation.5.clone | custom fusion | bytes 208896 | tf_op jit(solution)/shard_map/jit(_take)/gather | solution.py:98
  643.9 15.7 %psum.86 = f32[8]{0:T(128)S(1)} all-reduce(f32[8]{0:T(128)S(1)} %psum.85), channel_id=1, replica_groups=mesh['dev_0'=4,'dev_1'=4,'dev_2'=4,'dev_3'=2] {'dev_2'}, use_global_device_ids=true, to_apply=%region_23.28 | all-reduce | flops 8 | bytes 64 | tf_op jit(solution)/shard_map/psum | solution.py:39
  667.6 29.1 %all-gather.3 = f32[128,1,56]{2,1,0:T(1,128)S(1)} all-gather(f32[1,1,56]{2,1,0:T(1,128)S(1)} %maximum_bitcast_fusion.1), channel_id=1, replica_groups=mesh['dev_0'=4,'dev_1'=4,'dev_2'=4,'dev_3'=2] {'dev_0','dev_1','dev_2','..., dimensions={0}, use_global_device_ids=true | all-gather | bytes 28896 | tf_op jit(solution)/shard_map/all_gather | solution.py:32
  713.2 12.2 %gather_fusion.15 = f32[3072,8]{1,0:T(8,128)} fusion(f32[8,3072]{0,1:T(8,128)} %copy.195, s32[3072]{0:T(1024)S(1)} %get-tuple-element.246), kind=kCustom, calls=%fused_computation.6.clone | custom fusion | bytes 208896 | tf_op jit(solution)/shard_map/jit(_take)/gather | solution.py:98
  741.3 12.3 %gather_fusion.16 = f32[3072,8]{1,0:T(8,128)} fusion(f32[8,3073]{0,1:T(8,128)} %concatenate.79.clone, s32[3072]{0:T(1024)S(1)} %get-tuple-element.247), kind=kCustom, calls=%fused_computation.13.clone | custom fusion | bytes 208896 | tf_op jit(solution)/shard_map/jit(_take)/gather | solution.py:90
  778.6 12.2 %gather_fusion.17 = f32[3072,8]{1,0:T(8,128)} fusion(f32[8,3072]{0,1:T(8,128)} %bitcast_multiply_fusion.1, s32[3072]{0:T(1024)S(1)} %get-tuple-element.246), kind=kCustom, calls=%fused_computation.7.clone | custom fusion | bytes 208896 | tf_op jit(solution)/shard_map/jit(_take)/gather | solution.py:98
  804.9 17.9 %psum.90 = f32[8]{0:T(128)S(1)} all-reduce(f32[8]{0:T(128)S(1)} %psum.89), channel_id=1, replica_groups=mesh['dev_0'=4,'dev_1'=4,'dev_2'=4,'dev_3'=2] {'dev_2'}, use_global_device_ids=true, to_apply=%region_31.36 | all-reduce | flops 8 | bytes 64 | tf_op jit(solution)/shard_map/psum | solution.py:39
  830.6 29.1 %all-gather.4 = f32[128,1,56]{2,1,0:T(1,128)S(1)} all-gather(f32[1,1,56]{2,1,0:T(1,128)S(1)} %maximum_bitcast_fusion.2), channel_id=1, replica_groups=mesh['dev_0'=4,'dev_1'=4,'dev_2'=4,'dev_3'=2] {'dev_0','dev_1','dev_2','..., dimensions={0}, use_global_device_ids=true | all-gather | bytes 28896 | tf_op jit(solution)/shard_map/all_gather | solution.py:32
  877.2 12.2 %gather_fusion.18 = f32[3072,8]{1,0:T(8,128)} fusion(f32[8,3072]{0,1:T(8,128)} %copy.210, s32[3072]{0:T(1024)S(1)} %get-tuple-element.246), kind=kCustom, calls=%fused_computation.8.clone | custom fusion | bytes 208896 | tf_op jit(solution)/shard_map/jit(_take)/gather | solution.py:98
  906.0 12.3 %gather_fusion.19 = f32[3072,8]{1,0:T(8,128)} fusion(f32[8,3073]{0,1:T(8,128)} %concatenate.81.clone, s32[3072]{0:T(1024)S(1)} %get-tuple-element.247), kind=kCustom, calls=%fused_computation.14.clone | custom fusion | bytes 208896 | tf_op jit(solution)/shard_map/jit(_take)/gather | solution.py:90
  974.7 17.9 %psum.94 = f32[8]{0:T(128)S(1)} all-reduce(f32[8]{0:T(128)S(1)} %psum.93), channel_id=1, replica_groups=mesh['dev_0'=4,'dev_1'=4,'dev_2'=4,'dev_3'=2] {'dev_2'}, use_global_device_ids=true, to_apply=%region_39.44 | all-reduce | flops 8 | bytes 64 | tf_op jit(solution)/shard_map/psum | solution.py:39
  1001.8 29.1 %all-gather.5 = f32[128,1,56]{2,1,0:T(1,128)S(1)} all-gather(f32[1,1,56]{2,1,0:T(1,128)S(1)} %maximum_bitcast_fusion.3), channel_id=1, replica_groups=mesh['dev_0'=4,'dev_1'=4,'dev_2'=4,'dev_3'=2] {'dev_0','dev_1','dev_2','..., dimensions={0}, use_global_device_ids=true | all-gather | bytes 28896 | tf_op jit(solution)/shard_map/all_gather | solution.py:32
  (573 shorter events, 598.4 us)
Async XLA Ops:
  7.2 129.4 %all-gather.8.cloned.1.call-start = ((), (), s32[]{:S(2)}) async-start(), calls=%async_computation | async-start | bytes 3170304 | tf_op jit(solution)/shard_map/all_gather | solution.py:126
  41.3 25.2 %collective-permute-start.5 = (f32[6,512]{1,0:T(8,128)S(1)}, f32[6,512]{1,0:T(8,128)S(1)}, u32[]{:S(2)}, u32[]{:S(2)}) collective-permute-start(f32[6,512]{1,0:T(8,128)S(1)} %get-tuple-element.155), channel_id=1, source_target_pairs={{0,112},{1,113},{2,114},{3,115},{4,116},{5,117},{6,118},{7,119},{8... | collective-permute-start | bytes 36872 | tf_op jit(solution)/shard_map/ppermute | solution.py:24
  47.3 19.1 %collective-permute-start.4 = (f32[6,512]{1,0:T(8,128)S(1)}, f32[6,512]{1,0:T(8,128)S(1)}, u32[]{:S(2)}, u32[]{:S(2)}) collective-permute-start(f32[6,512]{1,0:T(8,128)S(1)} %get-tuple-element.156), channel_id=1, source_target_pairs={{0,16},{1,17},{2,18},{3,19},{4,20},{5,21},{6,22},{7,23},{8,24},{9,... | collective-permute-start | bytes 36872 | tf_op jit(solution)/shard_map/ppermute | solution.py:24
  47.3 19.1 %collective-permute-start.3 = (f32[6,512]{1,0:T(8,128)S(1)}, f32[6,512]{1,0:T(8,128)S(1)}, u32[]{:S(2)}, u32[]{:S(2)}) collective-permute-start(f32[6,512]{1,0:T(8,128)S(1)} %get-tuple-element.157), channel_id=1, source_target_pairs={{0,124},{1,125},{2,126},{3,127},{4,0},{5,1},{6,2},{7,3},{8,4},{9,5... | collective-permute-start | bytes 36872 | tf_op jit(solution)/shard_map/ppermute | solution.py:24
  55.5 11.0 %collective-permute-start.2 = (f32[6,512]{1,0:T(8,128)S(1)}, f32[6,512]{1,0:T(8,128)S(1)}, u32[]{:S(2)}, u32[]{:S(2)}) collective-permute-start(f32[6,512]{1,0:T(8,128)S(1)} %get-tuple-element.158), channel_id=1, source_target_pairs={{0,4},{1,5},{2,6},{3,7},{4,8},{5,9},{6,10},{7,11},{8,12},{9,13},{1... | collective-permute-start | bytes 36872 | tf_op jit(solution)/shard_map/ppermute | solution.py:24
  417.9 45.5 %collective-permute-start.11 = (f32[8,512]{1,0:T(8,128)S(1)}, f32[8,512]{1,0:T(8,128)S(1)}, u32[]{:S(2)}, u32[]{:S(2)}) collective-permute-start(f32[8,512]{1,0:T(8,128)S(1)} %get-tuple-element.143), channel_id=1, source_target_pairs={{0,112},{1,113},{2,114},{3,115},{4,116},{5,117},{6,118},{7,119},{8... | collective-permute-start | bytes 49160 | tf_op jit(solution)/shard_map/ppermute | solution.py:24
  421.1 27.9 %collective-permute-start.10 = (f32[8,512]{1,0:T(8,128)S(1)}, f32[8,512]{1,0:T(8,128)S(1)}, u32[]{:S(2)}, u32[]{:S(2)}) collective-permute-start(f32[8,512]{1,0:T(8,128)S(1)} %get-tuple-element.144), channel_id=1, source_target_pairs={{0,16},{1,17},{2,18},{3,19},{4,20},{5,21},{6,22},{7,23},{8,24},{9,... | collective-permute-start | bytes 49160 | tf_op jit(solution)/shard_map/ppermute | solution.py:24
  421.3 27.6 %collective-permute-start.9 = (f32[8,512]{1,0:T(8,128)S(1)}, f32[8,512]{1,0:T(8,128)S(1)}, u32[]{:S(2)}, u32[]{:S(2)}) collective-permute-start(f32[8,512]{1,0:T(8,128)S(1)} %get-tuple-element.145), channel_id=1, source_target_pairs={{0,124},{1,125},{2,126},{3,127},{4,0},{5,1},{6,2},{7,3},{8,4},{9,5... | collective-permute-start | bytes 49160 | tf_op jit(solution)/shard_map/ppermute | solution.py:24
  426.8 19.2 %collective-permute-start.8 = (f32[8,512]{1,0:T(8,128)S(1)}, f32[8,512]{1,0:T(8,128)S(1)}, u32[]{:S(2)}, u32[]{:S(2)}) collective-permute-start(f32[8,512]{1,0:T(8,128)S(1)} %get-tuple-element.146), channel_id=1, source_target_pairs={{0,4},{1,5},{2,6},{3,7},{4,8},{5,9},{6,10},{7,11},{8,12},{9,13},{1... | collective-permute-start | bytes 49160 | tf_op jit(solution)/shard_map/ppermute | solution.py:24
  437.2 8.8 collective-permute-start.7
  445.9 15.9 %collective-permute-start.17 = (f32[8,512]{1,0:T(8,128)S(1)}, f32[8,512]{1,0:T(8,128)S(1)}, u32[]{:S(2)}, u32[]{:S(2)}) collective-permute-start(f32[8,512]{1,0:T(8,128)S(1)} %get-tuple-element.149), channel_id=1, source_target_pairs={{0,112},{1,113},{2,114},{3,115},{4,116},{5,117},{6,118},{7,119},{8... | collective-permute-start | bytes 49160 | tf_op jit(solution)/shard_map/ppermute | solution.py:24
  445.9 15.8 %collective-permute-start.16 = (f32[8,512]{1,0:T(8,128)S(1)}, f32[8,512]{1,0:T(8,128)S(1)}, u32[]{:S(2)}, u32[]{:S(2)}) collective-permute-start(f32[8,512]{1,0:T(8,128)S(1)} %get-tuple-element.150), channel_id=1, source_target_pairs={{0,16},{1,17},{2,18},{3,19},{4,20},{5,21},{6,22},{7,23},{8,24},{9,... | collective-permute-start | bytes 49160 | tf_op jit(solution)/shard_map/ppermute | solution.py:24
  448.9 12.9 %collective-permute-start.15 = (f32[8,512]{1,0:T(8,128)S(1)}, f32[8,512]{1,0:T(8,128)S(1)}, u32[]{:S(2)}, u32[]{:S(2)}) collective-permute-start(f32[8,512]{1,0:T(8,128)S(1)} %get-tuple-element.151), channel_id=1, source_target_pairs={{0,124},{1,125},{2,126},{3,127},{4,0},{5,1},{6,2},{7,3},{8,4},{9,5... | collective-permute-start | bytes 49160 | tf_op jit(solution)/shard_map/ppermute | solution.py:24
  594.1 10.4 collective-permute-start.18
  594.2 18.7 %collective-permute-start.23 = (f32[8,512]{1,0:T(8,128)S(1)}, f32[8,512]{1,0:T(8,128)S(1)}, u32[]{:S(2)}, u32[]{:S(2)}) collective-permute-start(f32[8,512]{1,0:T(8,128)S(1)} %get-tuple-element.137), channel_id=1, source_target_pairs={{0,112},{1,113},{2,114},{3,115},{4,116},{5,117},{6,118},{7,119},{8... | collective-permute-start | bytes 49160 | tf_op jit(solution)/shard_map/ppermute | solution.py:24
  598.7 14.2 %collective-permute-start.22 = (f32[8,512]{1,0:T(8,128)S(1)}, f32[8,512]{1,0:T(8,128)S(1)}, u32[]{:S(2)}, u32[]{:S(2)}) collective-permute-start(f32[8,512]{1,0:T(8,128)S(1)} %get-tuple-element.138), channel_id=1, source_target_pairs={{0,16},{1,17},{2,18},{3,19},{4,20},{5,21},{6,22},{7,23},{8,24},{9,... | collective-permute-start | bytes 49160 | tf_op jit(solution)/shard_map/ppermute | solution.py:24
  598.7 14.1 %collective-permute-start.21 = (f32[8,512]{1,0:T(8,128)S(1)}, f32[8,512]{1,0:T(8,128)S(1)}, u32[]{:S(2)}, u32[]{:S(2)}) collective-permute-start(f32[8,512]{1,0:T(8,128)S(1)} %get-tuple-element.139), channel_id=1, source_target_pairs={{0,124},{1,125},{2,126},{3,127},{4,0},{5,1},{6,2},{7,3},{8,4},{9,5... | collective-permute-start | bytes 49160 | tf_op jit(solution)/shard_map/ppermute | solution.py:24
  758.6 15.3 %collective-permute-start.29 = (f32[8,512]{1,0:T(8,128)S(1)}, f32[8,512]{1,0:T(8,128)S(1)}, u32[]{:S(2)}, u32[]{:S(2)}) collective-permute-start(f32[8,512]{1,0:T(8,128)S(1)} %get-tuple-element.131), channel_id=1, source_target_pairs={{0,112},{1,113},{2,114},{3,115},{4,116},{5,117},{6,118},{7,119},{8... | collective-permute-start | bytes 49160 | tf_op jit(solution)/shard_map/ppermute | solution.py:24
  759.7 14.1 %collective-permute-start.28 = (f32[8,512]{1,0:T(8,128)S(1)}, f32[8,512]{1,0:T(8,128)S(1)}, u32[]{:S(2)}, u32[]{:S(2)}) collective-permute-start(f32[8,512]{1,0:T(8,128)S(1)} %get-tuple-element.132), channel_id=1, source_target_pairs={{0,16},{1,17},{2,18},{3,19},{4,20},{5,21},{6,22},{7,23},{8,24},{9,... | collective-permute-start | bytes 49160 | tf_op jit(solution)/shard_map/ppermute | solution.py:24
  761.5 12.3 %collective-permute-start.27 = (f32[8,512]{1,0:T(8,128)S(1)}, f32[8,512]{1,0:T(8,128)S(1)}, u32[]{:S(2)}, u32[]{:S(2)}) collective-permute-start(f32[8,512]{1,0:T(8,128)S(1)} %get-tuple-element.133), channel_id=1, source_target_pairs={{0,124},{1,125},{2,126},{3,127},{4,0},{5,1},{6,2},{7,3},{8,4},{9,5... | collective-permute-start | bytes 49160 | tf_op jit(solution)/shard_map/ppermute | solution.py:24
  921.7 8.7 collective-permute-start.30
  923.2 17.3 %collective-permute-start.35 = (f32[8,512]{1,0:T(8,128)S(1)}, f32[8,512]{1,0:T(8,128)S(1)}, u32[]{:S(2)}, u32[]{:S(2)}) collective-permute-start(f32[8,512]{1,0:T(8,128)S(1)} %get-tuple-element.125), channel_id=1, source_target_pairs={{0,112},{1,113},{2,114},{3,115},{4,116},{5,117},{6,118},{7,119},{8... | collective-permute-start | bytes 49160 | tf_op jit(solution)/shard_map/ppermute | solution.py:24
  924.3 15.6 %collective-permute-start.34 = (f32[8,512]{1,0:T(8,128)S(1)}, f32[8,512]{1,0:T(8,128)S(1)}, u32[]{:S(2)}, u32[]{:S(2)}) collective-permute-start(f32[8,512]{1,0:T(8,128)S(1)} %get-tuple-element.126), channel_id=1, source_target_pairs={{0,16},{1,17},{2,18},{3,19},{4,20},{5,21},{6,22},{7,23},{8,24},{9,... | collective-permute-start | bytes 49160 | tf_op jit(solution)/shard_map/ppermute | solution.py:24
  926.3 12.9 %collective-permute-start.33 = (f32[8,512]{1,0:T(8,128)S(1)}, f32[8,512]{1,0:T(8,128)S(1)}, u32[]{:S(2)}, u32[]{:S(2)}) collective-permute-start(f32[8,512]{1,0:T(8,128)S(1)} %get-tuple-element.127), channel_id=1, source_target_pairs={{0,124},{1,125},{2,126},{3,127},{4,0},{5,1},{6,2},{7,3},{8,4},{9,5... | collective-permute-start | bytes 49160 | tf_op jit(solution)/shard_map/ppermute | solution.py:24
  (43 other events, 977.7 us)
Sparse Core Ops, SparseCore 0:
  68.7 67.7 all-gather.7
where the time goes:
time: 1070 us; the launch traced here: 1060 us
  local copies, waits for them, and re-layouts  344 us (32%)
  blocking collectives  255 us (24%)
  other arithmetic  218 us (20%)
  matrix products  94.3 us (9%)
  starting transfers between devices  79.4 us (7%)
  waiting for transfers between devices  52.6 us (5%)
  between operations  20.1 us (2%)
    gather x20, local copies, waits for them, and re-layouts, spread_back(): return jnp.take(flattened, dof_codes, axis=1) * shared_float[None]  140 us
    another operation x23, other arithmetic, per_device(): factor = jnp.linalg.cholesky(coarse_matrix)  124 us
    all_gather x4, blocking collectives, sent_together(): out = lax.all_gather(both, axis, axis=dim, tiled=True)  122 us
    psum x12, blocking collectives, one_axis_at_a_time(): value = lax.psum(value, axis)  95.5 us
    gather x12, local copies, waits for them, and re-layouts, gather_faces(): return jnp.take(padded, inverse, axis=1)  82.5 us
    ppermute x36, starting transfers between devices, from_behind(): lax.ppermute(value, axis, [(i, (i + by) % length) for i in range(length)])  79.3 us
    another operation x4, other arithmetic, solve_coarse(): lax.linalg.triangular_solve(factor, middle, left_side=True, lower=True, t...  61.6 us
    ppermute x36, waiting for transfers between devices, from_behind(): lax.ppermute(value, axis, [(i, (i + by) % length) for i in range(length)])  38.4 us
  transfers between devices with their start and end apart: 37, of which 14 were waited for; matrix products, arithmetic and copies ran while one was open for 2% of the time, Pallas kernels for 0%

commit v1 on v0

v1 whole, which is shorter than its diff:
```python
import functools

import jax
import jax.numpy as jnp
from jax import lax
from jax.experimental import pallas as pl
from jax.experimental.pallas import tpu as pltpu
from jax.sharding import PartitionSpec as P

FACES = 6
MODES = 6
CAP = 512
NMAX = 3072
LOADS = 8
CHUNKS = NMAX // 128
ITERS = 3
DEVICES = 128
OPPOSITE = (1, 0, 3, 2, 5, 4)
FACE_STEPS = (-1, 1, -4, 4, -16, 16)
HIGHEST = lax.Precision.HIGHEST
F32 = jnp.float32
BF16 = jnp.bfloat16
MESH = pl.DeviceIdType.MESH


def iota(shape, dim):
    return lax.broadcasted_iota(jnp.int32, shape, dim)


def lane_take(values, lanes):
    return jnp.take_along_axis(values, lanes, axis=1, mode="promise_in_bounds")


def permuted_chunk(src, index_row):
    index = jnp.broadcast_to(index_row, (8, 128))
    chunk = index >> 7
    lanes = index & 127
    out = jnp.zeros((8, 128), F32)
    for s in range(CHUNKS):
        piece = lane_take(src[:, s * 128 : (s + 1) * 128], lanes)
        out = jnp.where(chunk == s, piece, out)
    return out


def neighbour(me, step):
    return lax.rem(me + step + DEVICES, DEVICES)


def face_slice(face):
    return pl.ds(face * CAP, CAP)


def greet(partners):
    barrier = pltpu.get_barrier_semaphore()
    for partner in partners:
        pl.semaphore_signal(barrier, inc=1, device_id=(partner,), device_id_type=MESH)
    pl.semaphore_wait(barrier, len(partners))


def remote(src, dst, send, recv, device):
    return pltpu.make_async_remote_copy(
        src_ref=src, dst_ref=dst, send_sem=send, recv_sem=recv,
        device_id=(device,), device_id_type=MESH,
    )


def split3(x):
    hi = x.astype(BF16).astype(F32)
    rest = x - hi
    mid = rest.astype(BF16).astype(F32)
    return hi, mid, rest - mid


def setup_kernel(
    counts, links, map_ref, modes_ref, rhs_ref, goal_ref,
    rows_out, basis_out, modes_out, rhs_out, inverse_out,
    padded, own, far, basis, gathered,
    halo_send, halo_recv, y_send, y_recv, x_send, x_recv, z_send, z_recv, c_send, c_recv,
):
    me = lax.axis_index("dev")
    core = lax.rem(me, 2)
    z = lax.rem(me // 2, 4)
    x = lax.rem(me // 8, 4)
    y = me // 32

    def at(y_, x_, z_, c_):
        return ((y_ * 4 + x_) * 4 + z_) * 2 + c_

    def turn(value, by):
        return lax.rem(value + by, 4)

    partners = [neighbour(me, step) for step in FACE_STEPS]
    partners += [at(turn(y, j), x, z, core) for j in (1, 2, 3)]
    partners += [at(y, turn(x, j), z, core) for j in (1, 2, 3)]
    partners += [at(y, x, turn(z, j), core) for j in (1, 2, 3)]
    partners += [at(y, x, z, 1 - core)]
    greet(partners)

    codes = map_ref[...]
    high = jnp.where(codes >= 0, codes >> 7, -1)
    low = jnp.where(codes >= 0, codes & 127, -1)
    column = iota((32, NMAX), 1)
    here = jnp.broadcast_to(high, (32, NMAX)) == iota((32, NMAX), 0)
    coarse_digit = jnp.where(here, column >> 6, 0).astype(F32).astype(BF16)
    fine_digit = jnp.where(here, column & 63, 0).astype(F32).astype(BF16)
    spots = (
        jnp.broadcast_to(low, (128, NMAX)) == iota((128, NMAX), 0)
    ).astype(F32).astype(BF16)
    digits = lax.dot_general(
        jnp.concatenate([coarse_digit, fine_digit], axis=0), spots,
        (((1,), (1,)), ((), ())), preferred_element_type=F32,
    )
    inverse = (digits[:32] * 64.0 + digits[32:]).astype(jnp.int32)
    inverse_out[...] = inverse[:CHUNKS]

    padded[...] = jnp.zeros_like(padded)
    padded[0:MODES, :] = modes_ref[0]
    for r in range(CHUNKS):
        face = r // 4
        live = iota((8, 128), 1) + (r % 4) * 128 < counts[0, face]
        row = inverse_out[r : r + 1, :]
        own[0, :, r * 128 : (r + 1) * 128] = jnp.where(live, permuted_chunk(padded, row), 0.0)
        own[1, :, r * 128 : (r + 1) * 128] = jnp.where(live, permuted_chunk(rhs_ref.at[0], row), 0.0)

    copies = [
        remote(
            own.at[:, :, face_slice(face)], far.at[:, :, face_slice(OPPOSITE[face])],
            halo_send.at[face], halo_recv.at[OPPOSITE[face]], neighbour(me, FACE_STEPS[face]),
        )
        for face in range(FACES)
    ]
    for copy in copies:
        copy.start()
    basis[...] = jnp.zeros_like(basis)
    basis[48:56, :] = own[0]
    modes_out[...] = own[0]
    for copy in copies:
        copy.wait()
    for face in range(FACES):
        limit = jnp.where(links[0, face] >= 0, counts[0, face], 0)
        shared = iota((8, CAP), 1) < limit
        lanes = face_slice(face)
        basis[8 * face : 8 * face + 8, lanes] = jnp.where(shared, -far[0, :, lanes], 0.0)
        rhs_out[:, lanes] = own[1, :, lanes] - jnp.where(shared, far[1, :, lanes], 0.0)

    row_block = lax.dot_general(
        own[0], basis[...], (((1,), (1,)), ((), ())),
        precision=HIGHEST, preferred_element_type=F32,
    )
    row_block = jnp.where(iota((8, 128), 0) == 6, jnp.broadcast_to(goal_ref[...], (8, 128)), row_block)
    gathered[y, x, z, core] = row_block
    phases = (
        (y, y_send, y_recv, lambda: gathered.at[y, x, z, core], lambda k: at(k, x, z, core)),
        (x, x_send, x_recv, lambda: gathered.at[:, x, z, core], lambda k: at(y, k, z, core)),
        (z, z_send, z_recv, lambda: gathered.at[:, :, z, core], lambda k: at(y, x, k, core)),
    )
    for place, send, recv, part, device in phases:
        copies = [
            remote(part(), part(), send.at[j - 1], recv.at[j - 1], device(turn(place, j)))
            for j in (1, 2, 3)
        ]
        for copy in copies:
            copy.start()
        if place is y:
            top = basis[0:64, :]
            hi = top.astype(BF16)
            basis_out[0:64, :] = hi
            basis_out[64:128, :] = (top - hi.astype(F32)).astype(BF16)
            basis_out[128:192, :] = hi
        for copy in copies:
            copy.wait()
    copy = remote(
        gathered.at[:, :, :, core], gathered.at[:, :, :, core],
        c_send, c_recv, at(y, x, z, 1 - core),
    )
    copy.start()
    copy.wait()
    rows_out[...] = gathered[...].reshape(DEVICES * 8, 128)


def invert_together(blocks, layers):
    lane = iota((8, 128), 1)
    sub = iota((8, 128), 0)

    def node(n, carry):
        base = pl.multiple_of(n * 8, 8)
        results = []
        for layer in layers:
            panel = blocks[layer, pl.ds(base, 8), :]
            cols = [lane_take(panel, jnp.full((8, 128), base + k, jnp.int32)) for k in range(MODES)]
            inside = (lane >> 3) == n
            work = jnp.where(inside, jnp.where(lane - base == sub, 1.0, 0.0), panel)
            for k in range(MODES):
                inv = 1.0 / jnp.broadcast_to(cols[k][k : k + 1, :], (8, 128))
                lift = jnp.where(sub == k, cols[k] - 1.0, cols[k])
                work = work - lift * (jnp.broadcast_to(work[k : k + 1, :], (8, 128)) * inv)
                for j in range(k + 1, MODES):
                    cols[j] = cols[j] - lift * (jnp.broadcast_to(cols[j][k : k + 1, :], (8, 128)) * inv)
            results.append(work)
        for layer, work in zip(layers, results):
            inside = (lane >> 3) == n
            spread = [jnp.broadcast_to(work[k : k + 1, :], (8, 128)) for k in range(MODES)]
            for m in range(16):
                row = blocks[layer, m * 8 : (m + 1) * 8, :]
                out = jnp.where(inside, 0.0, row)
                for k in range(MODES):
                    out = out - lane_take(row, jnp.full((8, 128), base + k, jnp.int32)) * spread[k]
                blocks[layer, m * 8 : (m + 1) * 8, :] = out
            blocks[layer, pl.ds(base, 8), :] = work
        return carry

    lax.fori_loop(0, 16, node, 0)


def mm(a, b):
    return jnp.dot(a, b, precision=HIGHEST, preferred_element_type=F32)


def coarse_kernel(owner, links, place, rows, rows_kept_out, solver_out, blocks, up, down, fold, sel):
    lane = iota((8, 128), 1)
    sub = iota((8, 128), 0)
    offset = owner[0]
    me = place[0]

    def layer_rows(layer, carry):
        for n in range(16):
            slot = (layer * 16 + n + offset) & (DEVICES - 1)
            tile = rows[pl.ds(pl.multiple_of(slot * 8, 8), 8), :]
            real = sub < MODES
            apart = (lane >> 3) - n
            within = lane & 7
            face = jnp.where(apart == 0, 6, jnp.where(apart == -1, 0, jnp.where(
                apart == 1, 1, jnp.where(apart == -4, 2, jnp.where(apart == 4, 3, 7)))))
            linked = (face < 7) & real & (within < MODES)
            block = jnp.where(linked, lane_take(tile, face * 8 + within), 0.0)
            pad = (apart == 0) & (within == sub) & (sub >= MODES)
            blocks[layer, n * 8 : n * 8 + 8, :] = jnp.where(pad, 1.0, block)
            here = (apart == 0) & real & (within < MODES)
            up[layer, n * 8 : n * 8 + 8, :] = jnp.where(here, lane_take(tile, 40 + within), 0.0)
            down[layer, n * 8 : n * 8 + 8, :] = jnp.where(here, lane_take(tile, 32 + within), 0.0)
        return carry

    lax.fori_loop(0, 8, layer_rows, 0)

    own = (me - offset) & (DEVICES - 1)
    for f in range(7):
        target = own if f == 6 else links[0, f]
        for layer in range(8):
            hit = ((lane >> 3) + 16 * layer == target) & ((lane & 7) == sub) & (sub < MODES)
            sel[layer, 8 * f : 8 * f + 8, :] = jnp.where(hit, 1.0, 0.0)
    for layer in range(8):
        sel[layer, 56:64, :] = jnp.zeros((8, 128), F32)

    for k in range(3):
        low, high = k, 7 - k
        invert_together(blocks, (low, high))
        fold[low] = mm(blocks[low], up[low])
        fold[high] = mm(blocks[high], down[high])
        blocks[low + 1] = blocks[low + 1] - mm(down[low + 1], fold[low])
        blocks[high - 1] = blocks[high - 1] - mm(up[high - 1], fold[high])
        sel[low + 1] = sel[low + 1] - mm(sel[low], fold[low])
        sel[high - 1] = sel[high - 1] - mm(sel[high], fold[high])
    invert_together(blocks, (3,))
    fold[3] = mm(blocks[3], up[3])
    blocks[4] = blocks[4] - mm(down[4], fold[3])
    sel[4] = sel[4] - mm(sel[3], fold[3])
    invert_together(blocks, (4,))
    sel[4] = mm(sel[4], blocks[4])
    for k in range(3, -1, -1):
        sel[k] = mm(sel[k] - mm(sel[k + 1], down[k + 1]), blocks[k])
        if k < 3:
            j = 7 - k
            sel[j] = mm(sel[j] - mm(sel[j - 1], up[j - 1]), blocks[j])

    parts = []
    for layer in range(8):
        parts.append(jnp.concatenate(split3(sel[layer]), axis=0).astype(BF16))
    row = iota((128, 128), 0)
    col = iota((128, 128), 1)
    for k in range(MODES):
        total = jnp.zeros((192, 128), F32)
        for layer in range(8):
            slot = ((row >> 3) + 16 * layer + offset) & (DEVICES - 1)
            hot = jnp.where(((row & 7) == k) & (slot == col), 1.0, 0.0).astype(BF16)
            total = total + jnp.dot(parts[layer], hot, preferred_element_type=F32)
        values = total[0:64] + total[64:128] + total[128:192]
        hi = values.astype(BF16)
        solver_out[k * 64 : (k + 1) * 64, 0:128] = hi
        solver_out[k * 64 : (k + 1) * 64, 128:256] = hi
        solver_out[k * 64 : (k + 1) * 64, 256:384] = (values - hi.astype(F32)).astype(BF16)
    rows_kept_out[...] = rows[pl.ds(6, DEVICES, stride=8), :]


def cg_kernel(
    counts, links, map_ref, inverse, modes, rhs, basis, solver, goal, dual_hbm,
    lambda_out, residual_out,
    dual, vec, low_vec, prod, image, far, lam, direction, applied, coarse, live, omega, table,
    dual_sem, halo_send, halo_recv, near_send, near_recv, wide_send, wide_recv,
):
    me = lax.axis_index("dev")
    q = lax.rem(me, 8)
    h = me // 8
    near = [h * 8 + lax.rem(q + j, 8) for j in range(1, 8)]
    wide = [lax.rem(h + j, 16) * 8 + q for j in range(1, 16)]
    load = pltpu.make_async_copy(dual_hbm.at[0], dual, dual_sem)
    load.start()
    greet([neighbour(me, step) for step in FACE_STEPS] + near + wide)

    lane = iota((8, 128), 1)
    sub = iota((8, 128), 0)
    for face in range(FACES):
        spot = iota((8, CAP), 1)
        alive = jnp.where(spot < counts[0, face], 1.0, 0.0)
        limit = jnp.where(links[0, face] >= 0, counts[0, face], 0)
        both = jnp.where(spot < limit, 1.0, 0.0)
        live[:, face_slice(face)] = both
        omega[:, face_slice(face)] = alive - 0.5 * both

    def coarse_solve(table_rows):
        hi = table_rows.astype(BF16)
        lo = (table_rows - hi.astype(F32)).astype(BF16)
        stacked = jnp.concatenate([hi, lo, hi], axis=0)
        out = jnp.dot(solver[...], stacked, preferred_element_type=F32)
        total = jnp.zeros((64, 128), F32)
        for k in range(MODES):
            total = jnp.where((iota((64, 128), 1) & 15) == k, out[k * 64 : (k + 1) * 64], total)
        top = total.astype(BF16)
        rest = (total - top.astype(F32)).astype(BF16)
        pair = jnp.concatenate([top, rest], axis=1)
        triple = jnp.concatenate([pair, pair, pair], axis=0)
        group = jnp.where(
            ((iota((8, 256), 1) & 127) >> 4) == iota((8, 256), 0), 1.0, 0.0
        ).astype(BF16)
        return lax.dot_general(
            group, triple, (((1,), (1,)), ((), ())), preferred_element_type=F32
        )

    def expand(z3):
        top = z3.astype(BF16).astype(F32)
        packed = jnp.where(iota((8, 192), 1) < 128, top, z3 - top).astype(BF16)
        return jnp.dot(packed, basis[...], preferred_element_type=F32)

    def dual_apply():
        def to_columns(o, carry):
            lanes = pl.ds(pl.multiple_of(o * 128, 128), 128)
            low_vec[:, lanes] = permuted_chunk(vec, map_ref[:, lanes]).astype(BF16)
            return carry

        lax.fori_loop(0, CHUNKS, to_columns, 0)

        def product(n, carry):
            lanes = pl.ds(pl.multiple_of(n * 512, 512), 512)
            prod[:, lanes] = jnp.dot(low_vec[...], dual[:, lanes], preferred_element_type=F32)
            return carry

        lax.fori_loop(0, NMAX // 512, product, 0)

        def to_faces(r, carry):
            lanes = pl.ds(pl.multiple_of(r * 128, 128), 128)
            image[:, lanes] = permuted_chunk(prod, inverse[pl.ds(r, 1), :])
            return carry

        lax.fori_loop(0, CHUNKS, to_faces, 0)
        copies = [
            remote(
                image.at[:, face_slice(face)], far.at[:, face_slice(OPPOSITE[face])],
                halo_send.at[face], halo_recv.at[OPPOSITE[face]],
                neighbour(me, FACE_STEPS[face]),
            )
            for face in range(FACES)
        ]
        for copy in copies:
            copy.start()
        for copy in copies:
            copy.wait()
        shared = live[...]
        alive = omega[...] + 0.5 * shared
        prod[...] = jnp.where(alive > 0.0, image[...], 0.0) - jnp.where(shared > 0.0, far[...], 0.0)

    def gather_sums(parity, columns):
        tile = jnp.zeros((8, 128), F32)
        for k, values in enumerate(columns):
            tile = jnp.where((lane & 15) == k, values, tile)
        mine = jnp.sum(jnp.where((lane >> 4) == sub, tile, 0.0), axis=0, keepdims=True)
        table[parity, h, pl.ds(q, 1), :] = mine
        row = lambda: table.at[parity, h, pl.ds(q, 1), :]
        copies = [
            remote(row(), row(), near_send.at[parity, j], near_recv.at[parity, j], near[j])
            for j in range(7)
        ]
        for copy in copies:
            copy.start()
        for copy in copies:
            copy.wait()
        copies = [
            remote(
                table.at[parity, h], table.at[parity, h],
                wide_send.at[parity, j], wide_recv.at[parity, j], wide[j],
            )
            for j in range(15)
        ]
        for copy in copies:
            copy.start()
        for copy in copies:
            copy.wait()
        return table[parity].reshape(DEVICES, 128)

    def mode_sums(values):
        return [
            jnp.sum(modes[a : a + 1, :] * values, axis=1, keepdims=True) for a in range(MODES)
        ]

    def summed(left, right):
        return jnp.sum(omega[...] * left * right, axis=1, keepdims=True)

    def total_of(totals, k):
        return jnp.sum(jnp.where(lane == 16 * sub + k, totals, 0.0), axis=1, keepdims=True)

    start = expand(coarse_solve(goal[...]))
    lam[...] = start
    vec[...] = start
    load.wait()
    dual_apply()
    residual = rhs[...] - prod[...]
    z3 = coarse_solve(gather_sums(0, mode_sums(residual)))
    vec[...] = residual - expand(z3)
    direction[...] = jnp.zeros_like(direction)
    applied[...] = jnp.zeros_like(applied)
    coarse[...] = jnp.zeros_like(coarse)

    def iteration(step, carry):
        rho_old, curve_old = carry
        dual_apply()
        w = vec[...]
        columns = mode_sums(prod[...]) + [
            summed(w, w), summed(w, prod[...]), summed(w, applied[...]),
            summed(direction[...], prod[...]),
        ]
        rows = gather_sums(lax.rem(step, 2), columns)
        totals = jnp.broadcast_to(jnp.sum(rows, axis=0, keepdims=True), (8, 128))
        rho = total_of(totals, 6)
        ratio = rho / rho_old
        curve = (
            total_of(totals, 7) + ratio * (total_of(totals, 8) + total_of(totals, 9))
            + ratio * ratio * curve_old
        )
        length = rho / curve
        z3 = coarse_solve(rows) + ratio * coarse[...]
        coarse[...] = z3
        image_of = prod[...] + ratio * applied[...]
        applied[...] = image_of
        way = vec[...] + ratio * direction[...]
        direction[...] = way
        lam[...] = lam[...] + length * way
        vec[...] = vec[...] - length * (image_of - expand(z3))
        return rho, curve

    far_off = jnp.full((8, 1), jnp.inf, F32)
    lax.fori_loop(1, ITERS + 1, iteration, (far_off, jnp.zeros((8, 1), F32)))

    def to_outputs(o, carry):
        lanes = pl.ds(pl.multiple_of(o * 128, 128), 128)
        row = map_ref[:, lanes]
        lambda_out[0, :, lanes] = permuted_chunk(lam, row)
        residual_out[0, :, lanes] = permuted_chunk(vec, row)
        return carry

    lax.fori_loop(0, CHUNKS, to_outputs, 0)


VM = pl.BlockSpec(memory_space=pltpu.VMEM)
SM = pl.BlockSpec(memory_space=pltpu.SMEM)
DMA = pltpu.SemaphoreType.DMA


def sds(shape, dtype=F32):
    return jax.ShapeDtypeStruct(shape, dtype)


def per_device(
    dual_blocks, rigid_modes, dual_local, coarse_rhs,
    iface_sizes, neighbours, shared_counts, iface_map, owner,
):
    goal_row = jnp.pad(coarse_rhs[0].T, ((0, 0), (0, 16 - MODES))).reshape(1, 128)
    rows, basis, modes, rhs, inverse = pl.pallas_call(
        setup_kernel,
        out_shape=(
            sds((DEVICES * 8, 128)), sds((192, NMAX), BF16), sds((8, NMAX)), sds((8, NMAX)),
            sds((CHUNKS, 128), jnp.int32),
        ),
        in_specs=[SM, SM, VM, VM, VM, VM],
        out_specs=(VM,) * 5,
        scratch_shapes=[
            pltpu.VMEM((8, NMAX), F32), pltpu.VMEM((2, 8, NMAX), F32),
            pltpu.VMEM((2, 8, NMAX), F32), pltpu.VMEM((128, NMAX), F32),
            pltpu.VMEM((4, 4, 4, 2, 8, 128), F32),
            DMA((6,)), DMA((6,)), DMA((3,)), DMA((3,)), DMA((3,)), DMA((3,)),
            DMA((3,)), DMA((3,)), DMA, DMA,
        ],
        compiler_params=pltpu.CompilerParams(
            collective_id=0, has_side_effects=True, vmem_limit_bytes=40 << 20
        ),
        name="setup",
    )(shared_counts, neighbours, iface_map, rigid_modes, dual_local, goal_row)

    place = lax.axis_index("dev").astype(jnp.int32).reshape(1)
    goal, solver = pl.pallas_call(
        coarse_kernel,
        out_shape=(sds((DEVICES, 128)), sds((64 * MODES, 384), BF16)),
        in_specs=[SM, SM, SM, VM],
        out_specs=(VM, VM),
        scratch_shapes=[
            pltpu.VMEM((8, 128, 128), F32), pltpu.VMEM((8, 128, 128), F32),
            pltpu.VMEM((8, 128, 128), F32), pltpu.VMEM((8, 128, 128), F32),
            pltpu.VMEM((8, 64, 128), F32),
        ],
        compiler_params=pltpu.CompilerParams(vmem_limit_bytes=40 << 20),
        name="coarse",
    )(owner, neighbours, place, rows)

    return pl.pallas_call(
        cg_kernel,
        out_shape=(sds((1, LOADS, NMAX)), sds((1, LOADS, NMAX))),
        in_specs=[SM, SM] + [VM] * 7 + [pl.BlockSpec(memory_space=pl.ANY)],
        out_specs=(VM, VM),
        scratch_shapes=[
            pltpu.VMEM((NMAX, NMAX), BF16), pltpu.VMEM((8, NMAX), F32),
            pltpu.VMEM((8, NMAX), BF16),
        ] + [pltpu.VMEM((8, NMAX), F32)] * 6 + [
            pltpu.VMEM((8, 192), F32), pltpu.VMEM((8, NMAX), F32), pltpu.VMEM((8, NMAX), F32),
            pltpu.VMEM((2, 16, 8, 128), F32),
            DMA, DMA((6,)), DMA((6,)), DMA((2, 7)), DMA((2, 7)), DMA((2, 15)), DMA((2, 15)),
        ],
        compiler_params=pltpu.CompilerParams(
            collective_id=1, has_side_effects=True, vmem_limit_bytes=56 << 20
        ),
        name="gradients",
    )(
        shared_counts, neighbours, iface_map, inverse, modes, rhs, basis, solver, goal, dual_blocks
    )


def solution(mesh):
    in_specs = (
        P("dev", None, None), P("dev", None, None), P("dev", None, None), P("dev", None, None),
        P("dev"), P("dev", None), P("dev", None), P("dev", None), P(),
    )
    out_specs = (P("dev", None, None), P("dev", None, None))
    return jax.shard_map(
        per_device, mesh=mesh, in_specs=in_specs, out_specs=out_specs, check_vma=False
    )
```

time: 1070 us -> 195 us (0.18)
  local copies, waits for them, and re-layouts: 344 us -> 11.4 us
  blocking collectives: 255 us -> 0 us
  other arithmetic: 218 us -> 0 us
  Pallas kernels: 0 us -> 183 us
  matrix products: 94.3 us -> 0 us
  starting transfers between devices: 79.4 us -> 0 us
  waiting for transfers between devices: 52.6 us -> 0 us
  between operations: 20.1 us -> 0.71 us
    gather x38 -> x0, local copies, waits for them, and re-layouts: 230 us -> none  [the longest x20 140 us: spread_back(): return jnp.take(flattened, dof_codes, axis=1) * shared_float[None]]
    another operation x28 -> x0, other arithmetic: 187 us -> none  [the longest x23 124 us: per_device(): factor = jnp.linalg.cholesky(coarse_matrix)]
    pallas_call x0 -> x3, Pallas kernels: none -> 183 us  [the longest x1 99.4 us: per_device(): pl.pallas_call(cg_kernel, out_shape=(sds((1, LOADS, NMAX)), sds((1, LOADS...]
    all_gather x5 -> x0, blocking collectives: 160 us -> none  [the longest x4 122 us: sent_together(): out = lax.all_gather(both, axis, axis=dim, tiled=True)]
    psum x12 -> x0, blocking collectives: 95.5 us -> none  [one_axis_at_a_time(): value = lax.psum(value, axis)]
    ppermute x36 -> x0, starting transfers between devices: 79.3 us -> none  [from_behind(): lax.ppermute(value, axis, [(i, (i + by) % length) for i in range(length)])]
    dot_general x20 -> x0, matrix products: 56.3 us -> none  [the longest x4 35.7 us: dual_apply(): lax.dot_general(vector.astype(jnp.bfloat16), dual_blocks[0], (((1,), (1,)...]
    ppermute x36 -> x0, waiting for transfers between devices: 38.4 us -> none  [from_behind(): lax.ppermute(value, axis, [(i, (i + by) % length) for i in range(length)])]
  transfers between devices with their start and end apart: 37 -> 0, of which waited for: 14 -> 0; matrix products, arithmetic and copies ran while one was open for 2% -> 0% of each run, Pallas kernels for 0% -> 0%
where the time goes in v1:
time: 195 us
  Pallas kernels  183 us (94%)
  local copies, waits for them, and re-layouts  11.4 us (6%)
    pallas_call x1, Pallas kernels, per_device(): pl.pallas_call(cg_kernel, out_shape=(sds((1, LOADS, NMAX)), sds((1, LOADS...  99.4 us
    pallas_call x1, Pallas kernels, per_device(): pl.pallas_call(coarse_kernel, out_shape=(sds((DEVICES, 128)), sds((64 * M...  51.2 us
    pallas_call x1, Pallas kernels, per_device(): pl.pallas_call(setup_kernel, out_shape=(sds((DEVICES * 8, 128)), sds((192...  32.2 us
    unnamed x27, local copies, waits for them, and re-layouts  10.6 us

profile of v1, /device:TPU:1, one launch (start us, length us, event | category | flops | bytes accessed | tf_op | source)
XLA Modules:
  0.0 195.0 jit_solution(1020089913356908911)
XLA Ops:
  0.6 0.8 copy.14
  1.4 0.1 reshape.10.goal_ref
  1.5 0.9 copy.11.modes_ref
  2.4 0.0 copy-start.4
  2.4 0.9 copy-done.4
  3.3 0.0 copy-start.6
  3.3 0.7 copy-done.6
  4.0 0.7 copy-done.8
  4.7 0.7 copy-done.10
  5.3 32.2 %setup.1 = (f32[1024,128]{1,0:T(8,128)S(1)}, bf16[192,3072]{1,0:T(8,128)(2,1)S(1)}, f32[8,3072]{1,0:T(8,128)S(1)}, f32[8,3072]{1,0:T(8,128)S(1)}, s32[24,128]{1,0:T(8,128)S(1)}) custom-call(s32[1,6]{1,0:T(1,128)S(1)} %copy-done.10, s32[1,6]{1,0:T(1,128)S(1)} %copy-done.8, s32[1,3072]{1,0:T(1,128)S(1)} %copy-done.6, f32[1,6,3072]{2,1,0:T(8,128)S(1)} %copy.11.modes_ref, ...), custom_call_target="tpu_custom_call" | custom-call | tf_op jit(solution)/shard_map/setup/pallas_call | solution.py:485
  37.5 0.0 copy-start
  37.6 1.0 copy-done
  38.6 0.7 copy-done.9
  39.3 0.7 copy-done.11
  39.9 51.2 %coarse.1 = (f32[128,128]{1,0:T(8,128)S(1)}, bf16[384,384]{1,0:T(8,128)(2,1)S(1)}) custom-call(s32[128]{0:T(128)S(1)} %copy-done.11, s32[1,6]{1,0:T(1,128)S(1)} %copy-done.9, s32[1]{0:T(128)} %bitcast.1.place, f32[1024,128]{1,0:T(8,128)S(1)} %get-tuple-element.13.rows), custom_call_target="tpu_custom_call" | custom-call | tf_op jit(solution)/shard_map/coarse/pallas_call | solution.py:507
  91.1 0.0 copy-done.2
  91.1 0.0 copy-start.1
  91.1 0.7 copy-done.1
  91.9 0.6 copy-done.5
  92.5 0.0 copy-done.3
  92.5 0.0 copy-done.7
  92.5 99.4 %gradients.1 = (f32[1,8,3072]{2,1,0:T(8,128)}, f32[1,8,3072]{2,1,0:T(8,128)}) custom-call(s32[1,6]{1,0:T(1,128)} %counts.3, s32[1,6]{1,0:T(1,128)} %links.5, s32[1,3072]{1,0:T(1,128)} %map_ref.3, s32[24,128]{1,0:T(8,128)} %copy-done.7, f32[8,3072]{1,0:T(8,128)} %copy-done.2, f32[8,3072]{1,0:T(8,128)} %copy-done.3, bf16[192,3072]{1,0:T(8,128)(2,1)} %copy-done, ...), custom_call_target="tpu_custom_call" | custom-call | tf_op jit(solution)/shard_map/gradients/pallas_call | solution.py:521
  191.9 1.5 copy.17
  193.4 1.5 copy.18
  (9 shorter events, 0.0 us)
Async XLA Ops:
  2.4 0.9 copy-start.4
  3.3 0.7 copy-start.6
  4.0 0.7 copy-start.8
  4.7 0.7 copy-start.10
  37.5 1.0 copy-start
  38.6 52.5 %copy-start.2 = (f32[8,3072]{1,0:T(8,128)}, f32[8,3072]{1,0:T(8,128)S(1)}, u32[]{:S(2)}) copy-start(f32[8,3072]{1,0:T(8,128)S(1)} %get-tuple-element.10.modes) | copy-start | bytes 294916
  38.6 53.9 %copy-start.3 = (f32[8,3072]{1,0:T(8,128)}, f32[8,3072]{1,0:T(8,128)S(1)}, u32[]{:S(2)}) copy-start(f32[8,3072]{1,0:T(8,128)S(1)} %get-tuple-element.11.rhs) | copy-start | bytes 294916
  38.6 53.9 %copy-start.7 = (s32[24,128]{1,0:T(8,128)}, s32[24,128]{1,0:T(8,128)S(1)}, u32[]{:S(2)}) copy-start(s32[24,128]{1,0:T(8,128)S(1)} %get-tuple-element.9.inverse) | copy-start | bytes 36868
  38.6 0.7 copy-start.9
  39.3 0.7 copy-start.11
  91.1 0.7 copy-start.1
  91.8 0.6 copy-start.5

commit v2 on v1

--- a/solution.py
+++ b/solution.py
@@ -73,7 +73,7 @@
 
 def setup_kernel(
     counts, links, map_ref, modes_ref, rhs_ref, goal_ref,
-    rows_out, basis_out, modes_out, rhs_out, inverse_out,
+    rows_out, basis_out, modes_out, edge_out, rhs_out, inverse_out,
     padded, own, far, basis, gathered,
     halo_send, halo_recv, y_send, y_recv, x_send, x_recv, z_send, z_recv, c_send, c_recv,
 ):
@@ -140,7 +140,9 @@
         limit = jnp.where(links[0, face] >= 0, counts[0, face], 0)
         shared = iota((8, CAP), 1) < limit
         lanes = face_slice(face)
-        basis[8 * face : 8 * face + 8, lanes] = jnp.where(shared, -far[0, :, lanes], 0.0)
+        edge = jnp.where(shared, -far[0, :, lanes], 0.0)
+        basis[8 * face : 8 * face + 8, lanes] = edge
+        edge_out[:, lanes] = edge
         rhs_out[:, lanes] = own[1, :, lanes] - jnp.where(shared, far[1, :, lanes], 0.0)
 
     row_block = lax.dot_general(
@@ -292,19 +294,24 @@
 
 
 def cg_kernel(
-    counts, links, map_ref, inverse, modes, rhs, basis, solver, goal, dual_hbm,
+    counts, links, map_ref, inverse, modes, edge, rhs, basis, solver, goal, dual_hbm,
     lambda_out, residual_out,
     dual, vec, low_vec, prod, image, far, lam, direction, applied, coarse, live, omega, table,
-    dual_sem, halo_send, halo_recv, near_send, near_recv, wide_send, wide_recv,
+    dual_sem, halo_send, halo_recv, wide_send, wide_recv,
 ):
     me = lax.axis_index("dev")
-    q = lax.rem(me, 8)
-    h = me // 8
-    near = [h * 8 + lax.rem(q + j, 8) for j in range(1, 8)]
-    wide = [lax.rem(h + j, 16) * 8 + q for j in range(1, 16)]
     load = pltpu.make_async_copy(dual_hbm.at[0], dual, dual_sem)
     load.start()
-    greet([neighbour(me, step) for step in FACE_STEPS] + near + wide)
+    barrier = pltpu.get_barrier_semaphore()
+
+    def hello(j, carry):
+        pl.semaphore_signal(
+            barrier, inc=1, device_id=(lax.rem(me + j, DEVICES),), device_id_type=MESH
+        )
+        return carry
+
+    lax.fori_loop(1, DEVICES, hello, 0)
+    pl.semaphore_wait(barrier, DEVICES - 1)
 
     lane = iota((8, 128), 1)
     sub = iota((8, 128), 0)
@@ -316,14 +323,19 @@
         live[:, face_slice(face)] = both
         omega[:, face_slice(face)] = alive - 0.5 * both
 
-    def coarse_solve(table_rows):
-        hi = table_rows.astype(BF16)
-        lo = (table_rows - hi.astype(F32)).astype(BF16)
-        stacked = jnp.concatenate([hi, lo, hi], axis=0)
-        out = jnp.dot(solver[...], stacked, preferred_element_type=F32)
+    def coarse_solve(even, odd):
+        rows = jnp.concatenate([even, odd], axis=1)
+        hi = rows.astype(BF16)
+        lo = (rows - hi.astype(F32)).astype(BF16)
+        out = jnp.dot(
+            solver[...], jnp.concatenate([hi, lo, hi], axis=0), preferred_element_type=F32
+        )
         total = jnp.zeros((64, 128), F32)
+        place = iota((64, 128), 1) & 15
         for k in range(MODES):
-            total = jnp.where((iota((64, 128), 1) & 15) == k, out[k * 64 : (k + 1) * 64], total)
+            part = out[k * 64 : (k + 1) * 64]
+            total = jnp.where(place == k, part[:, :128], total)
+            total = jnp.where(place == k + 8, part[:, 128:], total)
         top = total.astype(BF16)
         rest = (total - top.astype(F32)).astype(BF16)
         pair = jnp.concatenate([top, rest], axis=1)
@@ -340,7 +352,17 @@
         packed = jnp.where(iota((8, 192), 1) < 128, top, z3 - top).astype(BF16)
         return jnp.dot(packed, basis[...], preferred_element_type=F32)
 
-    def dual_apply():
+    def halo(parity):
+        return [
+            remote(
+                image.at[:, face_slice(face)], far.at[parity, :, face_slice(OPPOSITE[face])],
+                halo_send.at[parity, face], halo_recv.at[parity, OPPOSITE[face]],
+                neighbour(me, FACE_STEPS[face]),
+            )
+            for face in range(FACES)
+        ]
+
+    def dual_apply(parity):
         def to_columns(o, carry):
             lanes = pl.ds(pl.multiple_of(o * 128, 128), 128)
             low_vec[:, lanes] = permuted_chunk(vec, map_ref[:, lanes]).astype(BF16)
@@ -357,87 +379,105 @@
 
         def to_faces(r, carry):
             lanes = pl.ds(pl.multiple_of(r * 128, 128), 128)
-            image[:, lanes] = permuted_chunk(prod, inverse[pl.ds(r, 1), :])
+            piece = permuted_chunk(prod, inverse[pl.ds(r, 1), :])
+            image[:, lanes] = jnp.where(omega[:, lanes] > 0.0, piece, 0.0)
             return carry
 
         lax.fori_loop(0, CHUNKS, to_faces, 0)
-        copies = [
+        for copy in halo(parity):
+            copy.start()
+
+    def assembled(parity):
+        for copy in halo(parity):
+            copy.wait()
+        return image[...] - live[...] * far[parity]
+
+    def slot_rows(slot):
+        return pl.ds(pl.multiple_of(slot * 4, 4), 4)
+
+    def share(parity, own, faces, extra):
+        tiles = []
+        for r in range(4):
+            columns = list(enumerate(own)) + [(6 + k, e) for k, e in enumerate(extra)]
+            if r > 0:
+                columns = list(enumerate(faces[2 * r - 2]))
+                columns += [(8 + k, e) for k, e in enumerate(faces[2 * r - 1])]
+            tile = jnp.zeros((8, 128), F32)
+            for k, values in columns:
+                tile = jnp.where((lane & 15) == k, values, tile)
+            tiles.append(jnp.sum(jnp.where((lane >> 4) == sub, tile, 0.0), axis=0, keepdims=True))
+        table[parity, slot_rows(me), :] = jnp.concatenate(tiles, axis=0)
+
+        def send(j, carry):
+            part = table.at[parity, slot_rows(me), :]
             remote(
-                image.at[:, face_slice(face)], far.at[:, face_slice(OPPOSITE[face])],
-                halo_send.at[face], halo_recv.at[OPPOSITE[face]],
-                neighbour(me, FACE_STEPS[face]),
-            )
-            for face in range(FACES)
-        ]
-        for copy in copies:
-            copy.start()
-        for copy in copies:
-            copy.wait()
-        shared = live[...]
-        alive = omega[...] + 0.5 * shared
-        prod[...] = jnp.where(alive > 0.0, image[...], 0.0) - jnp.where(shared > 0.0, far[...], 0.0)
-
-    def gather_sums(parity, columns):
-        tile = jnp.zeros((8, 128), F32)
-        for k, values in enumerate(columns):
-            tile = jnp.where((lane & 15) == k, values, tile)
-        mine = jnp.sum(jnp.where((lane >> 4) == sub, tile, 0.0), axis=0, keepdims=True)
-        table[parity, h, pl.ds(q, 1), :] = mine
-        row = lambda: table.at[parity, h, pl.ds(q, 1), :]
-        copies = [
-            remote(row(), row(), near_send.at[parity, j], near_recv.at[parity, j], near[j])
-            for j in range(7)
-        ]
-        for copy in copies:
-            copy.start()
-        for copy in copies:
-            copy.wait()
-        copies = [
-            remote(
-                table.at[parity, h], table.at[parity, h],
-                wide_send.at[parity, j], wide_recv.at[parity, j], wide[j],
-            )
-            for j in range(15)
-        ]
-        for copy in copies:
-            copy.start()
-        for copy in copies:
-            copy.wait()
-        return table[parity].reshape(DEVICES, 128)
+                part, part, wide_send.at[parity], wide_recv.at[parity], lax.rem(me + j, DEVICES)
+            ).start()
+            return carry
+
+        lax.fori_loop(1, DEVICES, send, 0)
+        most = table.at[parity, pl.ds(0, 4 * DEVICES - 4), :]
+        everything = remote(
+            most, most, wide_send.at[parity], wide_recv.at[parity], lax.rem(me + 1, DEVICES)
+        )
+        everything.wait()
+        first = table[parity, pl.ds(0, DEVICES, stride=4), :]
+        even, odd = first, jnp.zeros((DEVICES, 128), F32)
+        for r in range(3):
+            pair = table[parity, pl.ds(r + 1, DEVICES, stride=4), :]
+            even = even + pltpu.roll(pair, FACE_STEPS[2 * r] % DEVICES, 0)
+            odd = odd + pltpu.roll(pair, FACE_STEPS[2 * r + 1] % DEVICES, 0)
+        return first, even, odd
 
     def mode_sums(values):
         return [
             jnp.sum(modes[a : a + 1, :] * values, axis=1, keepdims=True) for a in range(MODES)
         ]
 
-    def summed(left, right):
-        return jnp.sum(omega[...] * left * right, axis=1, keepdims=True)
+    def face_sums(values):
+        return [
+            [
+                jnp.sum(
+                    edge[a : a + 1, face * CAP : (face + 1) * CAP]
+                    * values[:, face * CAP : (face + 1) * CAP],
+                    axis=1, keepdims=True,
+                )
+                for a in range(MODES)
+            ]
+            for face in range(FACES)
+        ]
+
+    def summed(product):
+        return jnp.sum(product, axis=1, keepdims=True)
 
     def total_of(totals, k):
         return jnp.sum(jnp.where(lane == 16 * sub + k, totals, 0.0), axis=1, keepdims=True)
 
-    start = expand(coarse_solve(goal[...]))
+    start = expand(coarse_solve(goal[...], jnp.zeros((DEVICES, 128), F32)))
     lam[...] = start
     vec[...] = start
     load.wait()
-    dual_apply()
-    residual = rhs[...] - prod[...]
-    z3 = coarse_solve(gather_sums(0, mode_sums(residual)))
-    vec[...] = residual - expand(z3)
+    dual_apply(0)
+    negative = -image[...]
+    _, even, odd = share(0, mode_sums(rhs[...] + negative), face_sums(negative), [])
+    z3 = coarse_solve(even, odd)
+    vec[...] = rhs[...] - assembled(0) - expand(z3)
     direction[...] = jnp.zeros_like(direction)
     applied[...] = jnp.zeros_like(applied)
     coarse[...] = jnp.zeros_like(coarse)
 
     def iteration(step, carry):
         rho_old, curve_old = carry
-        dual_apply()
+        parity = lax.rem(step, 2)
+        dual_apply(parity)
         w = vec[...]
-        columns = mode_sums(prod[...]) + [
-            summed(w, w), summed(w, prod[...]), summed(w, applied[...]),
-            summed(direction[...], prod[...]),
+        y = image[...]
+        extra = [
+            summed(omega[...] * w * w), summed(w * y), summed(omega[...] * w * applied[...]),
+            summed(direction[...] * y),
         ]
-        rows = gather_sums(lax.rem(step, 2), columns)
-        totals = jnp.broadcast_to(jnp.sum(rows, axis=0, keepdims=True), (8, 128))
+        first, even, odd = share(parity, mode_sums(y), face_sums(y), extra)
+        totals = jnp.broadcast_to(jnp.sum(first, axis=0, keepdims=True), (8, 128))
         rho = total_of(totals, 6)
         ratio = rho / rho_old
         curve = (
@@ -445,9 +485,9 @@
             + ratio * ratio * curve_old
         )
         length = rho / curve
-        z3 = coarse_solve(rows) + ratio * coarse[...]
+        z3 = coarse_solve(even, odd) + ratio * coarse[...]
         coarse[...] = z3
-        image_of = prod[...] + ratio * applied[...]
+        image_of = assembled(parity) + ratio * applied[...]
         applied[...] = image_of
         way = vec[...] + ratio * direction[...]
         direction[...] = way
@@ -482,14 +522,14 @@
     iface_sizes, neighbours, shared_counts, iface_map, owner,
 ):
     goal_row = jnp.pad(coarse_rhs[0].T, ((0, 0), (0, 16 - MODES))).reshape(1, 128)
-    rows, basis, modes, rhs, inverse = pl.pallas_call(
+    rows, basis, modes, edge, rhs, inverse = pl.pallas_call(
         setup_kernel,
         out_shape=(
             sds((DEVICES * 8, 128)), sds((192, NMAX), BF16), sds((8, NMAX)), sds((8, NMAX)),
-            sds((CHUNKS, 128), jnp.int32),
+            sds((8, NMAX)), sds((CHUNKS, 128), jnp.int32),
         ),
         in_specs=[SM, SM, VM, VM, VM, VM],
-        out_specs=(VM,) * 5,
+        out_specs=(VM,) * 6,
         scratch_shapes=[
             pltpu.VMEM((8, NMAX), F32), pltpu.VMEM((2, 8, NMAX), F32),
             pltpu.VMEM((2, 8, NMAX), F32), pltpu.VMEM((128, NMAX), F32),
@@ -521,22 +561,24 @@
     return pl.pallas_call(
         cg_kernel,
         out_shape=(sds((1, LOADS, NMAX)), sds((1, LOADS, NMAX))),
-        in_specs=[SM, SM] + [VM] * 7 + [pl.BlockSpec(memory_space=pl.ANY)],
+        in_specs=[SM, SM] + [VM] * 8 + [pl.BlockSpec(memory_space=pl.ANY)],
         out_specs=(VM, VM),
         scratch_shapes=[
             pltpu.VMEM((NMAX, NMAX), BF16), pltpu.VMEM((8, NMAX), F32),
             pltpu.VMEM((8, NMAX), BF16),
-        ] + [pltpu.VMEM((8, NMAX), F32)] * 6 + [
+        ] + [pltpu.VMEM((8, NMAX), F32)] * 2 + [pltpu.VMEM((2, 8, NMAX), F32)]
+        + [pltpu.VMEM((8, NMAX), F32)] * 3 + [
             pltpu.VMEM((8, 192), F32), pltpu.VMEM((8, NMAX), F32), pltpu.VMEM((8, NMAX), F32),
-            pltpu.VMEM((2, 16, 8, 128), F32),
-            DMA, DMA((6,)), DMA((6,)), DMA((2, 7)), DMA((2, 7)), DMA((2, 15)), DMA((2, 15)),
+            pltpu.VMEM((2, 4 * DEVICES, 128), F32),
+            DMA, DMA((2, 6)), DMA((2, 6)), DMA((2,)), DMA((2,)),
         ],
         compiler_params=pltpu.CompilerParams(
             collective_id=1, has_side_effects=True, vmem_limit_bytes=56 << 20
         ),
         name="gradients",
     )(
-        shared_counts, neighbours, iface_map, inverse, modes, rhs, basis, solver, goal, dual_blocks
+        shared_counts, neighbours, iface_map, inverse, modes, edge, rhs, basis, solver, goal,
+        dual_blocks,
     )
 
 

time: 195 us -> 175 us (0.90)
  Pallas kernels: 183 us -> 162 us
    pallas_call x1, Pallas kernels: 99.4 us -> 78.8 us  [per_device(): pl.pallas_call(cg_kernel, out_shape=(sds((1, LOADS, NMAX)), sds((1, LOADS...]
    unnamed x27 -> x29, local copies, waits for them, and re-layouts: 10.6 us -> 10.6 us
where the time goes in v2:
time: 175 us; the launch traced here: 174 us
  Pallas kernels  162 us (93%)
  local copies, waits for them, and re-layouts  11.4 us (7%)
    pallas_call x1, Pallas kernels, per_device(): pl.pallas_call(cg_kernel, out_shape=(sds((1, LOADS, NMAX)), sds((1, LOADS...  78.8 us
    pallas_call x1, Pallas kernels, per_device(): pl.pallas_call(coarse_kernel, out_shape=(sds((DEVICES, 128)), sds((64 * M...  51.2 us
    pallas_call x1, Pallas kernels, per_device(): pl.pallas_call(setup_kernel, out_shape=(sds((DEVICES * 8, 128)), sds((192...  32.2 us
    unnamed x29, local copies, waits for them, and re-layouts  10.6 us

profile of v2, /device:TPU:1, one launch (start us, length us, event | category | flops | bytes accessed | tf_op | source)
XLA Modules:
  0.0 174.4 jit_solution(14884714142838297911)
XLA Ops:
  0.6 0.8 copy.14
  1.4 0.1 reshape.10.goal_ref
  1.5 0.9 copy.11.modes_ref
  2.4 0.0 copy-start.5
  2.4 0.9 copy-done.5
  3.3 0.7 copy-done.7
  4.0 0.7 copy-done.9
  4.7 0.7 copy-done.11
  5.3 32.2 %setup.1 = (f32[1024,128]{1,0:T(8,128)S(1)}, bf16[192,3072]{1,0:T(8,128)(2,1)S(1)}, f32[8,3072]{1,0:T(8,128)S(1)}, f32[8,3072]{1,0:T(8,128)S(1)}, f32[8,3072]{1,0:T(8,128)S(1)}, /*index=5*/s32[24,128]{1,0:T(8,128)S(1)}) custom-call(s32[1,6]{1,0:T(1,128)S(1)} %copy-done.11, s32[1,6]{1,0:T(1,128)S(1)} %copy-done.9, s32[1,3072]{1,0:T(1,128)S(1)} %copy-done.7, ...), custom_call_target="tpu_custom_call" | custom-call | tf_op jit(solution)/shard_map/setup/pallas_call | solution.py:525
  37.5 0.0 copy-start
  37.6 1.0 copy-done
  38.6 0.0 copy-start.10
  38.6 0.7 copy-done.10
  39.3 0.7 copy-done.12
  39.9 51.2 %coarse.1 = (f32[128,128]{1,0:T(8,128)S(1)}, bf16[384,384]{1,0:T(8,128)(2,1)S(1)}) custom-call(s32[128]{0:T(128)S(1)} %copy-done.12, s32[1,6]{1,0:T(1,128)S(1)} %copy-done.10, s32[1]{0:T(128)} %bitcast.1.place, f32[1024,128]{1,0:T(8,128)S(1)} %get-tuple-element.15.rows), custom_call_target="tpu_custom_call" | custom-call | tf_op jit(solution)/shard_map/coarse/pallas_call | solution.py:547
  91.1 0.0 copy-done.2
  91.1 0.0 copy-start.1
  91.1 0.7 copy-done.1
  91.8 0.6 copy-done.6
  92.5 0.0 copy-done.3
  92.5 0.0 copy-done.4
  92.5 78.8 %gradients.1 = (f32[1,8,3072]{2,1,0:T(8,128)}, f32[1,8,3072]{2,1,0:T(8,128)}) custom-call(s32[1,6]{1,0:T(1,128)} %counts.3, s32[1,6]{1,0:T(1,128)} %links.5, s32[1,3072]{1,0:T(1,128)} %map_ref.3, s32[24,128]{1,0:T(8,128)} %copy-done.8, f32[8,3072]{1,0:T(8,128)} %copy-done.2, f32[8,3072]{1,0:T(8,128)} %copy-done.3, f32[8,3072]{1,0:T(8,128)} %copy-done.4, ...), custom_call_target="tpu_custom_call" | custom-call | tf_op jit(solution)/shard_map/gradients/pallas_call | solution.py:561
  171.3 1.5 copy.17
  172.8 1.5 copy.18
  (11 shorter events, 0.0 us)
Async XLA Ops:
  2.4 0.9 copy-start.5
  3.3 0.7 copy-start.7
  4.0 0.7 copy-start.9
  4.7 0.7 copy-start.11
  37.5 1.0 copy-start
  38.6 52.5 %copy-start.2 = (f32[8,3072]{1,0:T(8,128)}, f32[8,3072]{1,0:T(8,128)S(1)}, u32[]{:S(2)}) copy-start(f32[8,3072]{1,0:T(8,128)S(1)} %get-tuple-element.11.modes) | copy-start | bytes 294916
  38.6 53.9 %copy-start.3 = (f32[8,3072]{1,0:T(8,128)}, f32[8,3072]{1,0:T(8,128)S(1)}, u32[]{:S(2)}) copy-start(f32[8,3072]{1,0:T(8,128)S(1)} %get-tuple-element.12.edge) | copy-start | bytes 294916
  38.6 53.9 %copy-start.4 = (f32[8,3072]{1,0:T(8,128)}, f32[8,3072]{1,0:T(8,128)S(1)}, u32[]{:S(2)}) copy-start(f32[8,3072]{1,0:T(8,128)S(1)} %get-tuple-element.13.rhs) | copy-start | bytes 294916
  38.6 53.9 %copy-start.8 = (s32[24,128]{1,0:T(8,128)}, s32[24,128]{1,0:T(8,128)S(1)}, u32[]{:S(2)}) copy-start(s32[24,128]{1,0:T(8,128)S(1)} %get-tuple-element.10.inverse) | copy-start | bytes 36868
  38.6 0.7 copy-start.10
  39.3 0.7 copy-start.12
  91.1 0.7 copy-start.1
  91.8 0.6 copy-start.6

commit v3 on v2

--- a/solution.py
+++ b/solution.py
@@ -14,6 +14,7 @@
 LOADS = 8
 CHUNKS = NMAX // 128
 ITERS = 3
+GROUP = 4
 DEVICES = 128
 OPPOSITE = (1, 0, 3, 2, 5, 4)
 FACE_STEPS = (-1, 1, -4, 4, -16, 16)
@@ -50,11 +51,17 @@
     return pl.ds(face * CAP, CAP)
 
 
-def greet(partners):
+def greet_all(me):
     barrier = pltpu.get_barrier_semaphore()
-    for partner in partners:
-        pl.semaphore_signal(barrier, inc=1, device_id=(partner,), device_id_type=MESH)
-    pl.semaphore_wait(barrier, len(partners))
+
+    def hello(j, carry):
+        pl.semaphore_signal(
+            barrier, inc=1, device_id=(lax.rem(me + j, DEVICES),), device_id_type=MESH
+        )
+        return carry
+
+    lax.fori_loop(1, DEVICES, hello, 0)
+    pl.semaphore_wait(barrier, DEVICES - 1)
 
 
 def remote(src, dst, send, recv, device):
@@ -74,27 +81,10 @@
 def setup_kernel(
     counts, links, map_ref, modes_ref, rhs_ref, goal_ref,
     rows_out, basis_out, modes_out, edge_out, rhs_out, inverse_out,
-    padded, own, far, basis, gathered,
-    halo_send, halo_recv, y_send, y_recv, x_send, x_recv, z_send, z_recv, c_send, c_recv,
+    padded, own, far, basis, gathered, halo_send, halo_recv, wide_send, wide_recv,
 ):
     me = lax.axis_index("dev")
-    core = lax.rem(me, 2)
-    z = lax.rem(me // 2, 4)
-    x = lax.rem(me // 8, 4)
-    y = me // 32
-
-    def at(y_, x_, z_, c_):
-        return ((y_ * 4 + x_) * 4 + z_) * 2 + c_
-
-    def turn(value, by):
-        return lax.rem(value + by, 4)
-
-    partners = [neighbour(me, step) for step in FACE_STEPS]
-    partners += [at(turn(y, j), x, z, core) for j in (1, 2, 3)]
-    partners += [at(y, turn(x, j), z, core) for j in (1, 2, 3)]
-    partners += [at(y, x, turn(z, j), core) for j in (1, 2, 3)]
-    partners += [at(y, x, z, 1 - core)]
-    greet(partners)
+    greet_all(me)
 
     codes = map_ref[...]
     high = jnp.where(codes >= 0, codes >> 7, -1)
@@ -150,68 +140,73 @@
         precision=HIGHEST, preferred_element_type=F32,
     )
     row_block = jnp.where(iota((8, 128), 0) == 6, jnp.broadcast_to(goal_ref[...], (8, 128)), row_block)
-    gathered[y, x, z, core] = row_block
-    phases = (
-        (y, y_send, y_recv, lambda: gathered.at[y, x, z, core], lambda k: at(k, x, z, core)),
-        (x, x_send, x_recv, lambda: gathered.at[:, x, z, core], lambda k: at(y, k, z, core)),
-        (z, z_send, z_recv, lambda: gathered.at[:, :, z, core], lambda k: at(y, x, k, core)),
-    )
-    for place, send, recv, part, device in phases:
-        copies = [
-            remote(part(), part(), send.at[j - 1], recv.at[j - 1], device(turn(place, j)))
-            for j in (1, 2, 3)
-        ]
-        for copy in copies:
-            copy.start()
-        if place is y:
-            top = basis[0:64, :]
-            hi = top.astype(BF16)
-            basis_out[0:64, :] = hi
-            basis_out[64:128, :] = (top - hi.astype(F32)).astype(BF16)
-            basis_out[128:192, :] = hi
-        for copy in copies:
-            copy.wait()
-    copy = remote(
-        gathered.at[:, :, :, core], gathered.at[:, :, :, core],
-        c_send, c_recv, at(y, x, z, 1 - core),
-    )
-    copy.start()
-    copy.wait()
-    rows_out[...] = gathered[...].reshape(DEVICES * 8, 128)
+    mine = pl.ds(pl.multiple_of(me * 8, 8), 8)
+    gathered[mine, :] = row_block
+
+    def send(j, carry):
+        part = gathered.at[mine, :]
+        remote(part, part, wide_send, wide_recv, lax.rem(me + j, DEVICES)).start()
+        return carry
+
+    lax.fori_loop(1, DEVICES, send, 0)
+    top = basis[0:64, :]
+    hi = top.astype(BF16)
+    basis_out[0:64, :] = hi
+    basis_out[64:128, :] = (top - hi.astype(F32)).astype(BF16)
+    basis_out[128:192, :] = hi
+    most = gathered.at[pl.ds(0, 8 * DEVICES - 8), :]
+    remote(most, most, wide_send, wide_recv, lax.rem(me + 1, DEVICES)).wait()
+    rows_out[...] = gathered[...]
 
 
 def invert_together(blocks, layers):
     lane = iota((8, 128), 1)
     sub = iota((8, 128), 0)
 
-    def node(n, carry):
-        base = pl.multiple_of(n * 8, 8)
+    def spread(values, k):
+        return jnp.broadcast_to(values[k : k + 1, :], (8, 128))
+
+    def pair(n, carry):
+        base = pl.multiple_of(n * 16, 16)
+        pivots = [(half, k) for half in range(2) for k in range(MODES)]
+        picks = [jnp.full((8, 128), base + 8 * half + k, jnp.int32) for half, k in pivots]
+        group = lane >> 4
+        inside = group == n
+        panels = [
+            [blocks[layer, pl.ds(base + 8 * half, 8), :] for half in range(2)] for layer in layers
+        ]
         results = []
-        for layer in layers:
-            panel = blocks[layer, pl.ds(base, 8), :]
-            cols = [lane_take(panel, jnp.full((8, 128), base + k, jnp.int32)) for k in range(MODES)]
-            inside = (lane >> 3) == n
-            work = jnp.where(inside, jnp.where(lane - base == sub, 1.0, 0.0), panel)
-            for k in range(MODES):
-                inv = 1.0 / jnp.broadcast_to(cols[k][k : k + 1, :], (8, 128))
-                lift = jnp.where(sub == k, cols[k] - 1.0, cols[k])
-                work = work - lift * (jnp.broadcast_to(work[k : k + 1, :], (8, 128)) * inv)
-                for j in range(k + 1, MODES):
-                    cols[j] = cols[j] - lift * (jnp.broadcast_to(cols[j][k : k + 1, :], (8, 128)) * inv)
-            results.append(work)
-        for layer, work in zip(layers, results):
-            inside = (lane >> 3) == n
-            spread = [jnp.broadcast_to(work[k : k + 1, :], (8, 128)) for k in range(MODES)]
-            for m in range(16):
-                row = blocks[layer, m * 8 : (m + 1) * 8, :]
-                out = jnp.where(inside, 0.0, row)
-                for k in range(MODES):
-                    out = out - lane_take(row, jnp.full((8, 128), base + k, jnp.int32)) * spread[k]
-                blocks[layer, m * 8 : (m + 1) * 8, :] = out
-            blocks[layer, pl.ds(base, 8), :] = work
+        for panel in panels:
+            cols = [[lane_take(part, pick) for part in panel] for pick in picks]
+            work = [
+                jnp.where(inside, jnp.where(lane - base == sub + 8 * half, 1.0, 0.0), panel[half])
+                for half in range(2)
+            ]
+            for p, (half, k) in enumerate(pivots):
+                inv = 1.0 / spread(cols[p][half], k)
+                lift = list(cols[p])
+                lift[half] = jnp.where(sub == k, lift[half] - 1.0, lift[half])
+                lift = [part * inv for part in lift]
+                for target in [work] + cols[p + 1 :]:
+                    row = spread(target[half], k)
+                    for other in range(2):
+                        target[other] = target[other] - lift[other] * row
+            results.append(jnp.concatenate(work, axis=0))
+        for layer, panel, work in zip(layers, panels, results):
+            column = jnp.concatenate([jnp.where(group < n, -part, part) for part in panel], axis=0)
+            a, b, c = split3(column)
+            d, e, f = split3(work)
+            left = jnp.concatenate([a, a, b, a, c, b], axis=0).astype(BF16)
+            right = jnp.concatenate([d, e, d, f, d, e], axis=0).astype(BF16)
+            change = lax.dot_general(
+                left, right, (((0,), (0,)), ((), ())), preferred_element_type=F32
+            )
+            clear = (iota((128, 128), 1) >> 4) == n
+            blocks[layer] = jnp.where(clear, 0.0, blocks[layer]) - change
+            blocks[layer, pl.ds(base, 16), :] = work
         return carry
 
-    lax.fori_loop(0, 16, node, 0)
+    lax.fori_loop(0, 8, pair, 0)
 
 
 def mm(a, b):
@@ -302,16 +297,7 @@
     me = lax.axis_index("dev")
     load = pltpu.make_async_copy(dual_hbm.at[0], dual, dual_sem)
     load.start()
-    barrier = pltpu.get_barrier_semaphore()
-
-    def hello(j, carry):
-        pl.semaphore_signal(
-            barrier, inc=1, device_id=(lax.rem(me + j, DEVICES),), device_id_type=MESH
-        )
-        return carry
-
-    lax.fori_loop(1, DEVICES, hello, 0)
-    pl.semaphore_wait(barrier, DEVICES - 1)
+    greet_all(me)
 
     lane = iota((8, 128), 1)
     sub = iota((8, 128), 0)
@@ -364,11 +350,12 @@
 
     def dual_apply(parity):
         def to_columns(o, carry):
-            lanes = pl.ds(pl.multiple_of(o * 128, 128), 128)
-            low_vec[:, lanes] = permuted_chunk(vec, map_ref[:, lanes]).astype(BF16)
+            for g in range(GROUP):
+                lanes = pl.ds(pl.multiple_of((o * GROUP + g) * 128, 128), 128)
+                low_vec[:, lanes] = permuted_chunk(vec, map_ref[:, lanes]).astype(BF16)
             return carry
 
-        lax.fori_loop(0, CHUNKS, to_columns, 0)
+        lax.fori_loop(0, CHUNKS // GROUP, to_columns, 0)
 
         def product(n, carry):
             lanes = pl.ds(pl.multiple_of(n * 512, 512), 512)
@@ -377,13 +364,15 @@
 
         lax.fori_loop(0, NMAX // 512, product, 0)
 
-        def to_faces(r, carry):
-            lanes = pl.ds(pl.multiple_of(r * 128, 128), 128)
-            piece = permuted_chunk(prod, inverse[pl.ds(r, 1), :])
-            image[:, lanes] = jnp.where(omega[:, lanes] > 0.0, piece, 0.0)
+        def to_faces(o, carry):
+            for g in range(GROUP):
+                r = o * GROUP + g
+                lanes = pl.ds(pl.multiple_of(r * 128, 128), 128)
+                piece = permuted_chunk(prod, inverse[pl.ds(r, 1), :])
+                image[:, lanes] = jnp.where(omega[:, lanes] > 0.0, piece, 0.0)
             return carry
 
-        lax.fori_loop(0, CHUNKS, to_faces, 0)
+        lax.fori_loop(0, CHUNKS // GROUP, to_faces, 0)
         for copy in halo(parity):
             copy.start()
 
@@ -499,13 +488,14 @@
     lax.fori_loop(1, ITERS + 1, iteration, (far_off, jnp.zeros((8, 1), F32)))
 
     def to_outputs(o, carry):
-        lanes = pl.ds(pl.multiple_of(o * 128, 128), 128)
-        row = map_ref[:, lanes]
-        lambda_out[0, :, lanes] = permuted_chunk(lam, row)
-        residual_out[0, :, lanes] = permuted_chunk(vec, row)
+        for g in range(GROUP):
+            lanes = pl.ds(pl.multiple_of((o * GROUP + g) * 128, 128), 128)
+            row = map_ref[:, lanes]
+            lambda_out[0, :, lanes] = permuted_chunk(lam, row)
+            residual_out[0, :, lanes] = permuted_chunk(vec, row)
         return carry
 
-    lax.fori_loop(0, CHUNKS, to_outputs, 0)
+    lax.fori_loop(0, CHUNKS // GROUP, to_outputs, 0)
 
 
 VM = pl.BlockSpec(memory_space=pltpu.VMEM)
@@ -533,9 +523,7 @@
         scratch_shapes=[
             pltpu.VMEM((8, NMAX), F32), pltpu.VMEM((2, 8, NMAX), F32),
             pltpu.VMEM((2, 8, NMAX), F32), pltpu.VMEM((128, NMAX), F32),
-            pltpu.VMEM((4, 4, 4, 2, 8, 128), F32),
-            DMA((6,)), DMA((6,)), DMA((3,)), DMA((3,)), DMA((3,)), DMA((3,)),
-            DMA((3,)), DMA((3,)), DMA, DMA,
+            pltpu.VMEM((DEVICES * 8, 128), F32), DMA((6,)), DMA((6,)), DMA, DMA,
         ],
         compiler_params=pltpu.CompilerParams(
             collective_id=0, has_side_effects=True, vmem_limit_bytes=40 << 20

time: 175 us -> 132 us (0.75)
  Pallas kernels: 162 us -> 120 us
    pallas_call x1, Pallas kernels: 51.2 us -> 21.9 us  [per_device(): pl.pallas_call(coarse_kernel, out_shape=(sds((DEVICES, 128)), sds((64 * M...]
    pallas_call x1, Pallas kernels: 78.8 us -> 68.8 us  [per_device(): pl.pallas_call(cg_kernel, out_shape=(sds((1, LOADS, NMAX)), sds((1, LOADS...]
    pallas_call x1, Pallas kernels: 32.2 us -> 28.9 us  [per_device(): pl.pallas_call(setup_kernel, out_shape=(sds((DEVICES * 8, 128)), sds((192...]
where the time goes in v3:
time: 132 us
  Pallas kernels  120 us (91%)
  local copies, waits for them, and re-layouts  11.4 us (9%)
    pallas_call x1, Pallas kernels, per_device(): pl.pallas_call(cg_kernel, out_shape=(sds((1, LOADS, NMAX)), sds((1, LOADS...  68.8 us
    pallas_call x1, Pallas kernels, per_device(): pl.pallas_call(setup_kernel, out_shape=(sds((DEVICES * 8, 128)), sds((192...  28.9 us
    pallas_call x1, Pallas kernels, per_device(): pl.pallas_call(coarse_kernel, out_shape=(sds((DEVICES, 128)), sds((64 * M...  21.9 us
    unnamed x29, local copies, waits for them, and re-layouts  10.6 us

profile of v3, /device:TPU:1, one launch (start us, length us, event | category | flops | bytes accessed | tf_op | source)
XLA Modules:
  0.0 131.7 jit_solution(17413156887055301059)
XLA Ops:
  0.6 0.8 copy.14
  1.4 0.1 reshape.10.goal_ref
  1.5 0.9 copy.11.modes_ref
  2.4 0.0 copy-start.5
  2.4 0.9 copy-done.5
  3.3 0.7 copy-done.7
  4.0 0.7 copy-done.9
  4.7 0.7 copy-done.11
  5.3 28.9 %setup.1 = (f32[1024,128]{1,0:T(8,128)S(1)}, bf16[192,3072]{1,0:T(8,128)(2,1)S(1)}, f32[8,3072]{1,0:T(8,128)S(1)}, f32[8,3072]{1,0:T(8,128)S(1)}, f32[8,3072]{1,0:T(8,128)S(1)}, /*index=5*/s32[24,128]{1,0:T(8,128)S(1)}) custom-call(s32[1,6]{1,0:T(1,128)S(1)} %copy-done.11, s32[1,6]{1,0:T(1,128)S(1)} %copy-done.9, s32[1,3072]{1,0:T(1,128)S(1)} %copy-done.7, ...), custom_call_target="tpu_custom_call" | custom-call | tf_op jit(solution)/shard_map/setup/pallas_call | solution.py:515
  34.2 0.0 copy-start
  34.2 1.0 copy-done
  35.2 0.0 copy-start.10
  35.2 0.7 copy-done.10
  35.9 0.7 copy-done.12
  36.6 21.9 %coarse.1 = (f32[128,128]{1,0:T(8,128)S(1)}, bf16[384,384]{1,0:T(8,128)(2,1)S(1)}) custom-call(s32[128]{0:T(128)S(1)} %copy-done.12, s32[1,6]{1,0:T(1,128)S(1)} %copy-done.10, s32[1]{0:T(128)} %bitcast.1.place, f32[1024,128]{1,0:T(8,128)S(1)} %get-tuple-element.15.rows), custom_call_target="tpu_custom_call" | custom-call | tf_op jit(solution)/shard_map/coarse/pallas_call | solution.py:535
  58.5 0.0 copy-done.2
  58.5 0.0 copy-start.1
  58.5 0.7 copy-done.1
  59.2 0.6 copy-done.6
  59.8 0.0 copy-done.3
  59.8 0.0 copy-done.4
  59.8 68.8 %gradients.1 = (f32[1,8,3072]{2,1,0:T(8,128)}, f32[1,8,3072]{2,1,0:T(8,128)}) custom-call(s32[1,6]{1,0:T(1,128)} %counts.3, s32[1,6]{1,0:T(1,128)} %links.5, s32[1,3072]{1,0:T(1,128)} %map_ref.3, s32[24,128]{1,0:T(8,128)} %copy-done.8, f32[8,3072]{1,0:T(8,128)} %copy-done.2, f32[8,3072]{1,0:T(8,128)} %copy-done.3, f32[8,3072]{1,0:T(8,128)} %copy-done.4, ...), custom_call_target="tpu_custom_call" | custom-call | tf_op jit(solution)/shard_map/gradients/pallas_call | solution.py:549
  128.6 1.5 %copy.17 = f32[1,8,3072]{2,1,0:T(8,128)} copy(f32[1,8,3072]{2,1,0:T(8,128)} %get-tuple-element.20) | data formatting | bytes 196608
  130.1 1.5 %copy.18 = f32[1,8,3072]{2,1,0:T(8,128)} copy(f32[1,8,3072]{2,1,0:T(8,128)} %get-tuple-element.21) | data formatting | bytes 196608
  (11 shorter events, 0.0 us)
Async XLA Ops:
  2.4 0.9 copy-start.5
  3.3 0.7 copy-start.7
  4.0 0.7 copy-start.9
  4.7 0.7 copy-start.11
  34.2 1.0 copy-start
  35.2 23.2 %copy-start.2 = (f32[8,3072]{1,0:T(8,128)}, f32[8,3072]{1,0:T(8,128)S(1)}, u32[]{:S(2)}) copy-start(f32[8,3072]{1,0:T(8,128)S(1)} %get-tuple-element.11.modes) | copy-start | bytes 294916
  35.2 24.6 %copy-start.3 = (f32[8,3072]{1,0:T(8,128)}, f32[8,3072]{1,0:T(8,128)S(1)}, u32[]{:S(2)}) copy-start(f32[8,3072]{1,0:T(8,128)S(1)} %get-tuple-element.12.edge) | copy-start | bytes 294916
  35.2 24.6 %copy-start.4 = (f32[8,3072]{1,0:T(8,128)}, f32[8,3072]{1,0:T(8,128)S(1)}, u32[]{:S(2)}) copy-start(f32[8,3072]{1,0:T(8,128)S(1)} %get-tuple-element.13.rhs) | copy-start | bytes 294916
  35.2 24.6 %copy-start.8 = (s32[24,128]{1,0:T(8,128)}, s32[24,128]{1,0:T(8,128)S(1)}, u32[]{:S(2)}) copy-start(s32[24,128]{1,0:T(8,128)S(1)} %get-tuple-element.10.inverse) | copy-start | bytes 36868
  35.2 0.7 copy-start.10
  35.9 0.7 copy-start.12
  58.5 0.7 copy-start.1
  59.2 0.6 copy-start.6

commit v4 on v3

--- a/solution.py
+++ b/solution.py
@@ -14,7 +14,7 @@
 LOADS = 8
 CHUNKS = NMAX // 128
 ITERS = 3
-GROUP = 4
+GROUP = 8
 DEVICES = 128
 OPPOSITE = (1, 0, 3, 2, 5, 4)
 FACE_STEPS = (-1, 1, -4, 4, -16, 16)
@@ -54,14 +54,24 @@
 def greet_all(me):
     barrier = pltpu.get_barrier_semaphore()
 
-    def hello(j, carry):
-        pl.semaphore_signal(
-            barrier, inc=1, device_id=(lax.rem(me + j, DEVICES),), device_id_type=MESH
-        )
+    to_everyone(me, lambda device: pl.semaphore_signal(
+        barrier, inc=1, device_id=(device,), device_id_type=MESH
+    ))
+
+
+def slot_rows(slot):
+    return pl.ds(pl.multiple_of(slot * 4, 4), 4)
+
+
+def to_everyone(me, act):
+    act(lax.rem(me + 1, DEVICES))
+
+    def some(j, carry):
+        for g in range(9):
+            act(lax.rem(me + 2 + 9 * j + g, DEVICES))
         return carry
 
-    lax.fori_loop(1, DEVICES, hello, 0)
-    pl.semaphore_wait(barrier, DEVICES - 1)
+    lax.fori_loop(0, 14, some, 0)
 
 
 def remote(src, dst, send, recv, device):
@@ -78,14 +88,12 @@
     return hi, mid, rest - mid
 
 
-def setup_kernel(
-    counts, links, map_ref, modes_ref, rhs_ref, goal_ref,
-    rows_out, basis_out, modes_out, edge_out, rhs_out, inverse_out,
-    padded, own, far, basis, gathered, halo_send, halo_recv, wide_send, wide_recv,
+def setup_part(
+    counts, links, map_ref, modes_ref, rhs_ref, goals,
+    gathered, basis_out, modes_out, edge_out, rhs_out, inverse_out,
+    padded, own, far, basis, halo_send, halo_recv, wide_send, wide_recv,
 ):
     me = lax.axis_index("dev")
-    greet_all(me)
-
     codes = map_ref[...]
     high = jnp.where(codes >= 0, codes >> 7, -1)
     low = jnp.where(codes >= 0, codes & 127, -1)
@@ -104,27 +112,33 @@
     inverse_out[...] = inverse[:CHUNKS]
 
     padded[...] = jnp.zeros_like(padded)
-    padded[0:MODES, :] = modes_ref[0]
+    for a in range(MODES):
+        padded[a : a + 1, :] = modes_ref[a]
     for r in range(CHUNKS):
         face = r // 4
         live = iota((8, 128), 1) + (r % 4) * 128 < counts[0, face]
         row = inverse_out[r : r + 1, :]
         own[0, :, r * 128 : (r + 1) * 128] = jnp.where(live, permuted_chunk(padded, row), 0.0)
-        own[1, :, r * 128 : (r + 1) * 128] = jnp.where(live, permuted_chunk(rhs_ref.at[0], row), 0.0)
-
-    copies = [
-        remote(
-            own.at[:, :, face_slice(face)], far.at[:, :, face_slice(OPPOSITE[face])],
-            halo_send.at[face], halo_recv.at[OPPOSITE[face]], neighbour(me, FACE_STEPS[face]),
-        )
-        for face in range(FACES)
-    ]
-    for copy in copies:
+        own[1, :, r * 128 : (r + 1) * 128] = jnp.where(live, permuted_chunk(rhs_ref, row), 0.0)
+
+    def exchange(which):
+        return [
+            remote(
+                own.at[which, :, face_slice(face)], far.at[which, :, face_slice(OPPOSITE[face])],
+                halo_send.at[which, face], halo_recv.at[which, OPPOSITE[face]],
+                neighbour(me, FACE_STEPS[face]),
+            )
+            for face in range(FACES)
+        ]
+
+    pl.semaphore_wait(pltpu.get_barrier_semaphore(), DEVICES - 1)
+    for copy in exchange(0) + exchange(1):
         copy.start()
     basis[...] = jnp.zeros_like(basis)
     basis[48:56, :] = own[0]
+    basis[112:120, :] = own[0]
     modes_out[...] = own[0]
-    for copy in copies:
+    for copy in exchange(0):
         copy.wait()
     for face in range(FACES):
         limit = jnp.where(links[0, face] >= 0, counts[0, face], 0)
@@ -132,31 +146,40 @@
         lanes = face_slice(face)
         edge = jnp.where(shared, -far[0, :, lanes], 0.0)
         basis[8 * face : 8 * face + 8, lanes] = edge
+        basis[8 * face + 64 : 8 * face + 72, lanes] = edge
         edge_out[:, lanes] = edge
-        rhs_out[:, lanes] = own[1, :, lanes] - jnp.where(shared, far[1, :, lanes], 0.0)
 
     row_block = lax.dot_general(
         own[0], basis[...], (((1,), (1,)), ((), ())),
         precision=HIGHEST, preferred_element_type=F32,
     )
-    row_block = jnp.where(iota((8, 128), 0) == 6, jnp.broadcast_to(goal_ref[...], (8, 128)), row_block)
-    mine = pl.ds(pl.multiple_of(me * 8, 8), 8)
-    gathered[mine, :] = row_block
-
-    def send(j, carry):
-        part = gathered.at[mine, :]
-        remote(part, part, wide_send, wide_recv, lax.rem(me + j, DEVICES)).start()
-        return carry
-
-    lax.fori_loop(1, DEVICES, send, 0)
+    spot = iota((1, 128), 1)
+    goal_row = jnp.zeros((1, 128), F32)
+    for a in range(MODES):
+        for l in range(LOADS):
+            goal_row = jnp.where(spot == 16 * l + a, goals[0, a * LOADS + l], goal_row)
+    packed = jnp.where(iota((3, 128), 1) < 64, row_block[0:3], row_block[3:6])
+    gathered[slot_rows(me), :] = jnp.concatenate([packed, goal_row], axis=0)
+
+    def start_send(device):
+        part = gathered.at[slot_rows(me), :]
+        remote(part, part, wide_send, wide_recv, device).start()
+
+    to_everyone(me, start_send)
     top = basis[0:64, :]
     hi = top.astype(BF16)
     basis_out[0:64, :] = hi
     basis_out[64:128, :] = (top - hi.astype(F32)).astype(BF16)
     basis_out[128:192, :] = hi
-    most = gathered.at[pl.ds(0, 8 * DEVICES - 8), :]
+    for copy in exchange(1):
+        copy.wait()
+    for face in range(FACES):
+        limit = jnp.where(links[0, face] >= 0, counts[0, face], 0)
+        shared = iota((8, CAP), 1) < limit
+        lanes = face_slice(face)
+        rhs_out[:, lanes] = own[1, :, lanes] - jnp.where(shared, far[1, :, lanes], 0.0)
+    most = gathered.at[pl.ds(0, 4 * DEVICES - 4), :]
     remote(most, most, wide_send, wide_recv, lax.rem(me + 1, DEVICES)).wait()
-    rows_out[...] = gathered[...]
 
 
 def invert_together(blocks, layers):
@@ -183,7 +206,9 @@
                 for half in range(2)
             ]
             for p, (half, k) in enumerate(pivots):
-                inv = 1.0 / spread(cols[p][half], k)
+                pivot = spread(cols[p][half], k)
+                inv = pl.reciprocal(pivot, approx=True)
+                inv = inv * (2.0 - pivot * inv)
                 lift = list(cols[p])
                 lift[half] = jnp.where(sub == k, lift[half] - 1.0, lift[half])
                 lift = [part * inv for part in lift]
@@ -213,28 +238,44 @@
     return jnp.dot(a, b, precision=HIGHEST, preferred_element_type=F32)
 
 
-def coarse_kernel(owner, links, place, rows, rows_kept_out, solver_out, blocks, up, down, fold, sel):
+def coarse_part(
+    owner, links, rows, rows_kept_out, solver_out, ordered, blocks, up, down, fold, sel,
+):
     lane = iota((8, 128), 1)
     sub = iota((8, 128), 0)
     offset = owner[0]
-    me = place[0]
+    me = lax.axis_index("dev")
+
+    turned = rows[...]
+    for bit in range(7):
+        by = 4 << bit
+        if by % 8:
+            moved = pltpu.roll(turned, 4 * DEVICES - by, 0)
+        else:
+            moved = jnp.concatenate([turned[by:], turned[:by]], axis=0)
+        turned = jnp.where(((offset >> bit) & 1) == 1, moved, turned)
+    ordered[...] = turned
 
     def layer_rows(layer, carry):
         for n in range(16):
-            slot = (layer * 16 + n + offset) & (DEVICES - 1)
-            tile = rows[pl.ds(pl.multiple_of(slot * 8, 8), 8), :]
+            slot = layer * 16 + n
+            tile = jnp.broadcast_to(ordered[pl.ds(slot * 4 + 2, 1), :], (8, 128))
+            for r in range(2):
+                part = jnp.broadcast_to(ordered[pl.ds(slot * 4 + r, 1), :], (8, 128))
+                tile = jnp.where((sub == r) | (sub == r + 3), part, tile)
+            aside = jnp.where(sub < 3, 0, 64)
             real = sub < MODES
             apart = (lane >> 3) - n
             within = lane & 7
             face = jnp.where(apart == 0, 6, jnp.where(apart == -1, 0, jnp.where(
                 apart == 1, 1, jnp.where(apart == -4, 2, jnp.where(apart == 4, 3, 7)))))
             linked = (face < 7) & real & (within < MODES)
-            block = jnp.where(linked, lane_take(tile, face * 8 + within), 0.0)
+            block = jnp.where(linked, lane_take(tile, ((face * 8 + within) & 63) + aside), 0.0)
             pad = (apart == 0) & (within == sub) & (sub >= MODES)
             blocks[layer, n * 8 : n * 8 + 8, :] = jnp.where(pad, 1.0, block)
             here = (apart == 0) & real & (within < MODES)
-            up[layer, n * 8 : n * 8 + 8, :] = jnp.where(here, lane_take(tile, 40 + within), 0.0)
-            down[layer, n * 8 : n * 8 + 8, :] = jnp.where(here, lane_take(tile, 32 + within), 0.0)
+            up[layer, n * 8 : n * 8 + 8, :] = jnp.where(here, lane_take(tile, 40 + within + aside), 0.0)
+            down[layer, n * 8 : n * 8 + 8, :] = jnp.where(here, lane_take(tile, 32 + within + aside), 0.0)
         return carry
 
     lax.fori_loop(0, 8, layer_rows, 0)
@@ -285,20 +326,16 @@
         solver_out[k * 64 : (k + 1) * 64, 0:128] = hi
         solver_out[k * 64 : (k + 1) * 64, 128:256] = hi
         solver_out[k * 64 : (k + 1) * 64, 256:384] = (values - hi.astype(F32)).astype(BF16)
-    rows_kept_out[...] = rows[pl.ds(6, DEVICES, stride=8), :]
-
-
-def cg_kernel(
-    counts, links, map_ref, inverse, modes, edge, rhs, basis, solver, goal, dual_hbm,
+    rows_kept_out[...] = rows[pl.ds(3, DEVICES, stride=4), :]
+
+
+def gradients_part(
+    counts, links, map_ref, inverse, modes, edge, rhs, basis, solver, goal, load,
     lambda_out, residual_out,
     dual, vec, low_vec, prod, image, far, lam, direction, applied, coarse, live, omega, table,
-    dual_sem, halo_send, halo_recv, wide_send, wide_recv,
+    halo_send, halo_recv, wide_send, wide_recv,
 ):
     me = lax.axis_index("dev")
-    load = pltpu.make_async_copy(dual_hbm.at[0], dual, dual_sem)
-    load.start()
-    greet_all(me)
-
     lane = iota((8, 128), 1)
     sub = iota((8, 128), 0)
     for face in range(FACES):
@@ -381,9 +418,6 @@
             copy.wait()
         return image[...] - live[...] * far[parity]
 
-    def slot_rows(slot):
-        return pl.ds(pl.multiple_of(slot * 4, 4), 4)
-
     def share(parity, own, faces, extra):
         tiles = []
         for r in range(4):
@@ -397,14 +431,11 @@
             tiles.append(jnp.sum(jnp.where((lane >> 4) == sub, tile, 0.0), axis=0, keepdims=True))
         table[parity, slot_rows(me), :] = jnp.concatenate(tiles, axis=0)
 
-        def send(j, carry):
+        def start_send(device):
             part = table.at[parity, slot_rows(me), :]
-            remote(
-                part, part, wide_send.at[parity], wide_recv.at[parity], lax.rem(me + j, DEVICES)
-            ).start()
-            return carry
-
-        lax.fori_loop(1, DEVICES, send, 0)
+            remote(part, part, wide_send.at[parity], wide_recv.at[parity], device).start()
+
+        to_everyone(me, start_send)
         most = table.at[parity, pl.ds(0, 4 * DEVICES - 4), :]
         everything = remote(
             most, most, wide_send.at[parity], wide_recv.at[parity], lax.rem(me + 1, DEVICES)
@@ -498,75 +529,80 @@
     lax.fori_loop(0, CHUNKS // GROUP, to_outputs, 0)
 
 
+def kernel(
+    counts, links, owner, goals, map_hbm, modes_hbm, rhs_hbm, dual_hbm,
+    lambda_out, residual_out,
+    map_in, modes_in, rhs_in, input_sems,
+    gathered, basis, modes, edge, rhs, inverse, padded, own, early_far, wide_basis,
+    early_send, early_recv, rows_send, rows_recv,
+    goal, solver, ordered, blocks, up, down, fold, sel,
+    dual, dual_sem, *scratch,
+):
+    greet_all(lax.axis_index("dev"))
+    inputs = [
+        pltpu.make_async_copy(map_hbm, map_in, input_sems.at[0]),
+        pltpu.make_async_copy(modes_hbm, modes_in, input_sems.at[1]),
+        pltpu.make_async_copy(rhs_hbm.at[0], rhs_in, input_sems.at[2]),
+    ]
+    for copy in inputs:
+        copy.start()
+    load = pltpu.make_async_copy(dual_hbm.at[0], dual, dual_sem)
+    load.start()
+    for copy in inputs:
+        copy.wait()
+    setup_part(
+        counts, links, map_in, modes_in, rhs_in, goals,
+        gathered, basis, modes, edge, rhs, inverse,
+        padded, own, early_far, wide_basis, early_send, early_recv, rows_send, rows_recv,
+    )
+    coarse_part(owner, links, gathered, goal, solver, ordered, blocks, up, down, fold, sel)
+    gradients_part(
+        counts, links, map_in, inverse, modes, edge, rhs, basis, solver, goal, load,
+        lambda_out, residual_out, dual, *scratch,
+    )
+
+
 VM = pl.BlockSpec(memory_space=pltpu.VMEM)
 SM = pl.BlockSpec(memory_space=pltpu.SMEM)
+ANY = pl.BlockSpec(memory_space=pl.ANY)
 DMA = pltpu.SemaphoreType.DMA
 
 
-def sds(shape, dtype=F32):
-    return jax.ShapeDtypeStruct(shape, dtype)
+def vmem(*shape, dtype=F32):
+    return pltpu.VMEM(shape, dtype)
 
 
 def per_device(
     dual_blocks, rigid_modes, dual_local, coarse_rhs,
     iface_sizes, neighbours, shared_counts, iface_map, owner,
 ):
-    goal_row = jnp.pad(coarse_rhs[0].T, ((0, 0), (0, 16 - MODES))).reshape(1, 128)
-    rows, basis, modes, edge, rhs, inverse = pl.pallas_call(
-        setup_kernel,
-        out_shape=(
-            sds((DEVICES * 8, 128)), sds((192, NMAX), BF16), sds((8, NMAX)), sds((8, NMAX)),
-            sds((8, NMAX)), sds((CHUNKS, 128), jnp.int32),
-        ),
-        in_specs=[SM, SM, VM, VM, VM, VM],
-        out_specs=(VM,) * 6,
+    out = jax.ShapeDtypeStruct((1, LOADS, NMAX), F32)
+    return pl.pallas_call(
+        kernel,
+        out_shape=(out, out),
+        in_specs=[SM] * 4 + [ANY] * 4,
+        out_specs=(VM, VM),
         scratch_shapes=[
-            pltpu.VMEM((8, NMAX), F32), pltpu.VMEM((2, 8, NMAX), F32),
-            pltpu.VMEM((2, 8, NMAX), F32), pltpu.VMEM((128, NMAX), F32),
-            pltpu.VMEM((DEVICES * 8, 128), F32), DMA((6,)), DMA((6,)), DMA, DMA,
+            vmem(1, NMAX, dtype=jnp.int32), vmem(MODES, 1, NMAX), vmem(8, NMAX), DMA((3,)),
+            vmem(DEVICES * 4, 128), vmem(192, NMAX, dtype=BF16), vmem(8, NMAX), vmem(8, NMAX),
+            vmem(8, NMAX), vmem(CHUNKS, 128, dtype=jnp.int32), vmem(8, NMAX), vmem(2, 8, NMAX),
+            vmem(2, 8, NMAX), vmem(128, NMAX), DMA((2, 6)), DMA((2, 6)), DMA, DMA,
+            vmem(DEVICES, 128), vmem(64 * MODES, 384, dtype=BF16), vmem(DEVICES * 4, 128),
+            vmem(8, 128, 128), vmem(8, 128, 128), vmem(8, 128, 128), vmem(8, 128, 128),
+            vmem(8, 64, 128),
+            vmem(NMAX, NMAX, dtype=BF16), DMA,
+            vmem(8, NMAX), vmem(8, NMAX, dtype=BF16), vmem(8, NMAX), vmem(8, NMAX),
+            vmem(2, 8, NMAX), vmem(8, NMAX), vmem(8, NMAX), vmem(8, NMAX), vmem(8, 192),
+            vmem(8, NMAX), vmem(8, NMAX), vmem(2, 4 * DEVICES, 128),
+            DMA((2, 6)), DMA((2, 6)), DMA((2,)), DMA((2,)),
         ],
         compiler_params=pltpu.CompilerParams(
-            collective_id=0, has_side_effects=True, vmem_limit_bytes=40 << 20
+            collective_id=0, has_side_effects=True, vmem_limit_bytes=58 << 20
         ),
-        name="setup",
-    )(shared_counts, neighbours, iface_map, rigid_modes, dual_local, goal_row)
-
-    place = lax.axis_index("dev").astype(jnp.int32).reshape(1)
-    goal, solver = pl.pallas_call(
-        coarse_kernel,
-        out_shape=(sds((DEVICES, 128)), sds((64 * MODES, 384), BF16)),
-        in_specs=[SM, SM, SM, VM],
-        out_specs=(VM, VM),
-        scratch_shapes=[
-            pltpu.VMEM((8, 128, 128), F32), pltpu.VMEM((8, 128, 128), F32),
-            pltpu.VMEM((8, 128, 128), F32), pltpu.VMEM((8, 128, 128), F32),
-            pltpu.VMEM((8, 64, 128), F32),
-        ],
-        compiler_params=pltpu.CompilerParams(vmem_limit_bytes=40 << 20),
-        name="coarse",
-    )(owner, neighbours, place, rows)
-
-    return pl.pallas_call(
-        cg_kernel,
-        out_shape=(sds((1, LOADS, NMAX)), sds((1, LOADS, NMAX))),
-        in_specs=[SM, SM] + [VM] * 8 + [pl.BlockSpec(memory_space=pl.ANY)],
-        out_specs=(VM, VM),
-        scratch_shapes=[
-            pltpu.VMEM((NMAX, NMAX), BF16), pltpu.VMEM((8, NMAX), F32),
-            pltpu.VMEM((8, NMAX), BF16),
-        ] + [pltpu.VMEM((8, NMAX), F32)] * 2 + [pltpu.VMEM((2, 8, NMAX), F32)]
-        + [pltpu.VMEM((8, NMAX), F32)] * 3 + [
-            pltpu.VMEM((8, 192), F32), pltpu.VMEM((8, NMAX), F32), pltpu.VMEM((8, NMAX), F32),
-            pltpu.VMEM((2, 4 * DEVICES, 128), F32),
-            DMA, DMA((2, 6)), DMA((2, 6)), DMA((2,)), DMA((2,)),
-        ],
-        compiler_params=pltpu.CompilerParams(
-            collective_id=1, has_side_effects=True, vmem_limit_bytes=56 << 20
-        ),
-        name="gradients",
+        name="feti",
     )(
-        shared_counts, neighbours, iface_map, inverse, modes, edge, rhs, basis, solver, goal,
-        dual_blocks,
+        shared_counts, neighbours, owner, coarse_rhs.reshape(1, MODES * LOADS), iface_map,
+        rigid_modes.transpose(1, 0, 2), dual_local, dual_blocks,
     )
 
 

time: 132 us -> 111 us (0.84)
  Pallas kernels: 120 us -> 106 us
  local copies, waits for them, and re-layouts: 11.4 us -> 3.67 us
    pallas_call x3 -> x1, Pallas kernels: 120 us -> 106 us  [per_device(): pl.pallas_call(kernel, out_shape=(out, out), in_specs=[SM] * 4 + [ANY] *...]
    unnamed x29 -> x2, local copies, waits for them, and re-layouts: 10.6 us -> 3.08 us
where the time goes in v4:
time: 111 us
  Pallas kernels  106 us (95%)
  local copies, waits for them, and re-layouts  3.67 us (3%)
    pallas_call x1, Pallas kernels, per_device(): pl.pallas_call(kernel, out_shape=(out, out), in_specs=[SM] * 4 + [ANY] *...  106 us
    unnamed x2, local copies, waits for them, and re-layouts  3.08 us

profile of v4, /device:TPU:1, one launch (start us, length us, event | category | flops | bytes accessed | tf_op | source)
XLA Modules:
  0.0 110.8 jit_solution(309727608683916809)
XLA Ops:
  0.6 0.7 reduce
  1.3 0.6 reshape.7.goals
  1.9 105.8 %feti.1 = (f32[1,8,3072]{2,1,0:T(8,128)}, f32[1,8,3072]{2,1,0:T(8,128)}) custom-call(s32[1,6]{1,0:T(1,128)} %counts.1, s32[1,6]{1,0:T(1,128)} %links.1, s32[128]{0:T(128)} %owner.1, f32[1,48]{1,0:T(1,128)} %reshape.7.goals, s32[1,3072]{1,0:T(1,128)} %map_hbm.1, f32[6,1,3072]{2,1,0:T(1,128)} %bitcast.1, f32[1,8,3072]{2,1,0:T(8,128)} %rhs_hbm.1, ...), custom_call_target="tpu_custom_call" | custom-call | tf_op jit(solution)/shard_map/feti/pallas_call | solution.py:580
  107.8 1.5 %copy.12 = f32[1,8,3072]{2,1,0:T(8,128)} copy(f32[1,8,3072]{2,1,0:T(8,128)} %get-tuple-element.4) | data formatting | bytes 196608
  109.3 1.5 %copy.13 = f32[1,8,3072]{2,1,0:T(8,128)} copy(f32[1,8,3072]{2,1,0:T(8,128)} %get-tuple-element.5) | data formatting | bytes 196608

commit v5 on v4

--- a/solution.py
+++ b/solution.py
@@ -14,7 +14,7 @@
 LOADS = 8
 CHUNKS = NMAX // 128
 ITERS = 3
-GROUP = 8
+GROUP = 12
 DEVICES = 128
 OPPOSITE = (1, 0, 3, 2, 5, 4)
 FACE_STEPS = (-1, 1, -4, 4, -16, 16)
@@ -64,14 +64,26 @@
 
 
 def to_everyone(me, act):
-    act(lax.rem(me + 1, DEVICES))
-
-    def some(j, carry):
-        for g in range(9):
-            act(lax.rem(me + 2 + 9 * j + g, DEVICES))
-        return carry
-
-    lax.fori_loop(0, 14, some, 0)
+    q = lax.rem(me, 8)
+    x = lax.rem(me // 8, 4)
+    y = me // 32
+
+    def at(dy, dx, dq):
+        return (lax.rem(y + dy, 4) * 4 + lax.rem(x + dx, 4)) * 8 + lax.rem(q + dq, 8)
+
+    order = (4, 5, 3, 2, 6, 1, 7, 0)
+    for dy in (2, 1, 3):
+
+        def some(i, carry, dy=dy):
+            for dq in order:
+                act(at(dy, i + 2, dq))
+            return carry
+
+        lax.fori_loop(0, 4, some, 0)
+    for dx in (2, 1, 3, 0):
+        for dq in order:
+            if dx or dq:
+                act(at(0, dx, dq))
 
 
 def remote(src, dst, send, recv, device):
@@ -157,7 +169,7 @@
     goal_row = jnp.zeros((1, 128), F32)
     for a in range(MODES):
         for l in range(LOADS):
-            goal_row = jnp.where(spot == 16 * l + a, goals[0, a * LOADS + l], goal_row)
+            goal_row = jnp.where(spot == 16 * l + a, goals[a, 0, l], goal_row)
     packed = jnp.where(iota((3, 128), 1) < 64, row_block[0:3], row_block[3:6])
     gathered[slot_rows(me), :] = jnp.concatenate([packed, goal_row], axis=0)
 
@@ -331,7 +343,7 @@
 
 def gradients_part(
     counts, links, map_ref, inverse, modes, edge, rhs, basis, solver, goal, load,
-    lambda_out, residual_out,
+    both_out,
     dual, vec, low_vec, prod, image, far, lam, direction, applied, coarse, live, omega, table,
     halo_send, halo_recv, wide_send, wide_recv,
 ):
@@ -522,8 +534,8 @@
         for g in range(GROUP):
             lanes = pl.ds(pl.multiple_of((o * GROUP + g) * 128, 128), 128)
             row = map_ref[:, lanes]
-            lambda_out[0, :, lanes] = permuted_chunk(lam, row)
-            residual_out[0, :, lanes] = permuted_chunk(vec, row)
+            both_out[0, :, lanes] = permuted_chunk(lam, row)
+            both_out[1, :, lanes] = permuted_chunk(vec, row)
         return carry
 
     lax.fori_loop(0, CHUNKS // GROUP, to_outputs, 0)
@@ -531,7 +543,7 @@
 
 def kernel(
     counts, links, owner, goals, map_hbm, modes_hbm, rhs_hbm, dual_hbm,
-    lambda_out, residual_out,
+    both_out,
     map_in, modes_in, rhs_in, input_sems,
     gathered, basis, modes, edge, rhs, inverse, padded, own, early_far, wide_basis,
     early_send, early_recv, rows_send, rows_recv,
@@ -558,7 +570,7 @@
     coarse_part(owner, links, gathered, goal, solver, ordered, blocks, up, down, fold, sel)
     gradients_part(
         counts, links, map_in, inverse, modes, edge, rhs, basis, solver, goal, load,
-        lambda_out, residual_out, dual, *scratch,
+        both_out, dual, *scratch,
     )
 
 
@@ -576,12 +588,12 @@
     dual_blocks, rigid_modes, dual_local, coarse_rhs,
     iface_sizes, neighbours, shared_counts, iface_map, owner,
 ):
-    out = jax.ShapeDtypeStruct((1, LOADS, NMAX), F32)
-    return pl.pallas_call(
+    out = jax.ShapeDtypeStruct((2, LOADS, NMAX), F32)
+    both = pl.pallas_call(
         kernel,
-        out_shape=(out, out),
+        out_shape=out,
         in_specs=[SM] * 4 + [ANY] * 4,
-        out_specs=(VM, VM),
+        out_specs=VM,
         scratch_shapes=[
             vmem(1, NMAX, dtype=jnp.int32), vmem(MODES, 1, NMAX), vmem(8, NMAX), DMA((3,)),
             vmem(DEVICES * 4, 128), vmem(192, NMAX, dtype=BF16), vmem(8, NMAX), vmem(8, NMAX),
@@ -601,9 +613,10 @@
         ),
         name="feti",
     )(
-        shared_counts, neighbours, owner, coarse_rhs.reshape(1, MODES * LOADS), iface_map,
+        shared_counts, neighbours, owner, coarse_rhs.transpose(1, 0, 2), iface_map,
         rigid_modes.transpose(1, 0, 2), dual_local, dual_blocks,
     )
+    return both[0:1], both[1:2]
 
 
 def solution(mesh):

time: 111 us -> 106 us (0.955)
  local copies, waits for them, and re-layouts: 3.67 us -> 1.63 us
  Pallas kernels: 106 us -> 104 us
    unnamed x2 -> x0, local copies, waits for them, and re-layouts: 3.08 us -> none
    pallas_call x1, Pallas kernels: 106 us -> 104 us  [per_device(): pl.pallas_call(kernel, out_shape=out, in_specs=[SM] * 4 + [ANY] * 4, out_...]
    slice x0 -> x1, local copies, waits for them, and re-layouts: none -> 1.63 us  [per_device(): return (both[0:1], both[1:2])]
where the time goes in v5:
time: 106 us
  Pallas kernels  104 us (98%)
  local copies, waits for them, and re-layouts  1.63 us (2%)
    pallas_call x1, Pallas kernels, per_device(): pl.pallas_call(kernel, out_shape=out, in_specs=[SM] * 4 + [ANY] * 4, out_...  104 us

profile of v5, /device:TPU:1, one launch (start us, length us, event | category | flops | bytes accessed | tf_op | source)
XLA Modules:
  0.0 105.8 jit_solution(6696048364018274737)
XLA Ops:
  0.6 103.5 %feti.1 = f32[2,8,3072]{2,1,0:T(8,128)} custom-call(s32[1,6]{1,0:T(1,128)} %counts.1, s32[1,6]{1,0:T(1,128)} %links.1, s32[128]{0:T(128)} %owner.1, f32[6,1,8]{2,1,0:T(1,128)} %bitcast.3, s32[1,3072]{1,0:T(1,128)} %map_hbm.1, f32[6,1,3072]{2,1,0:T(1,128)} %bitcast.2, f32[1,8,3072]{2,1,0:T(8,128)} %rhs_hbm.1, bf16[1,3072,3072]{2,1,0:T(8,128)(2,1)} %dual_hbm.1), custom_call_target="tpu_custom_call" | custom-call | tf_op jit(solution)/shard_map/feti/pallas_call | solution.py:592
  104.2 1.6 %fusion = (f32[1,8,3072]{2,1,0:T(8,128)}, f32[1,8,3072]{2,1,0:T(8,128)}) fusion(f32[2,8,3072]{2,1,0:T(8,128)} %feti.1), kind=kLoop, calls=%fused_computation | loop fusion | bytes 393216 | tf_op jit(solution)/shard_map/slice | solution.py:619
